TPU v7x, 32 devices: a whole 2x2x4 slice. The times are simulated.
32 devices in a mesh: data: 4 (over z), stage: 8 (over y, x, core).
Axes of the slice: x: 2, y: 2, z: 4, core: 2. Of those that a mesh axis runs over, the one named last changes fastest.
Arguments:
- w_in: float32 [8, 768, 3072], P('stage')
- w_out: float32 [8, 3072, 768], P('stage')
- mom_in: float32 [8, 768, 3072], P('stage')
- mom_out: float32 [8, 3072, 768], P('stage')
- sq_in: float32 [8, 768, 3072], P('stage')
- sq_out: float32 [8, 3072, 768], P('stage')
- acc_in: float32 [4, 8, 768, 3072], P('data', 'stage')
- acc_out: float32 [4, 8, 3072, 768], P('data', 'stage')
- stage_acts: bfloat16 [8, 256, 768], P('stage', 'data')
- grad_y: bfloat16 [256, 768], P('data')
- x_next: bfloat16 [1, 256, 768], P(None, 'data')
- max_norm: float32 [], replicated
Outputs:
- output 1: float32 [8, 768, 3072], P('stage')
- output 2: float32 [8, 3072, 768], P('stage')
- output 3: float32 [8, 768, 3072], P('stage')
- output 4: float32 [8, 3072, 768], P('stage')
- output 5: float32 [8, 768, 3072], P('stage')
- output 6: float32 [8, 3072, 768], P('stage')
- output 7: bfloat16 [1, 256, 768], P(None, 'data')
All inputs are finite; a program needn't handle non-finite values.
Results may differ from a plain program's by a relative error of at most 0.0138451.
Values are sent between devices in bfloat16 or wider.
A program may use at most 1 GiB of HBM per device.

v0:
```python
import jax
import jax.numpy as jnp
from jax import lax
from jax.sharding import PartitionSpec as P

BETA_ONE = 0.9
BETA_TWO = 0.95
ADAM_EPS = 1e-8
WEIGHT_DECAY = 0.1
LR_GAIN = 0.2
CLIP_EPS = 1e-6
STEP_COUNT = 20


def gelu_back(pre_act, grad_h):
    return jax.vjp(jax.nn.gelu, pre_act)[1](grad_h)[0]


def stage_forward(x_in, w_first, w_second):
    pre_act = jnp.einsum('nd,df->nf', x_in, w_first, preferred_element_type=jnp.float32)
    hidden = jax.nn.gelu(pre_act).astype(jnp.bfloat16)
    return jnp.einsum('nf,fd->nd', hidden, w_second, preferred_element_type=jnp.float32).astype(jnp.bfloat16)


def adamw_update(weight, moment, sq_moment, gradient, learn_rate):
    moment_new = BETA_ONE * moment + (1.0 - BETA_ONE) * gradient
    sq_new = BETA_TWO * sq_moment + (1.0 - BETA_TWO) * gradient * gradient
    m_hat = moment_new / (1.0 - BETA_ONE ** STEP_COUNT)
    v_hat = sq_new / (1.0 - BETA_TWO ** STEP_COUNT)
    weight_new = weight * (1.0 - learn_rate * WEIGHT_DECAY) - learn_rate * m_hat / (jnp.sqrt(v_hat) + ADAM_EPS)
    return weight_new, moment_new, sq_new


def solution(mesh):
    stages = mesh.shape['stage']
    replicas = mesh.shape['data']
    to_prev = [(idx, idx - 1) for idx in range(1, stages)]
    to_next = [(idx, idx + 1) for idx in range(stages - 1)]
    weight_spec = P('stage', None, None)
    acc_spec = P('data', 'stage', None, None)

    def local_step(w_in, w_out, mom_in, mom_out, sq_in, sq_out, acc_in, acc_out, stage_acts, grad_y, x_next, max_norm):
        stage_idx = lax.axis_index('stage')
        w_first = w_in[0].astype(jnp.bfloat16)
        w_second = w_out[0].astype(jnp.bfloat16)
        x_saved = stage_acts[0]
        tok_rows = grad_y.shape[0]
        ff_width = w_first.shape[1]

        def back_active(carry):
            grad_cur = carry[0]
            pre_act = jnp.einsum('nd,df->nf', x_saved, w_first, preferred_element_type=jnp.float32)
            hidden = jax.nn.gelu(pre_act).astype(jnp.bfloat16)
            grad_h = jnp.einsum('nd,fd->nf', grad_cur, w_second, preferred_element_type=jnp.float32)
            grad_pre = gelu_back(pre_act, grad_h).astype(jnp.bfloat16)
            grad_next = jnp.einsum('nf,df->nd', grad_pre, w_first, preferred_element_type=jnp.float32).astype(jnp.bfloat16)
            return grad_next, grad_cur, hidden, grad_pre

        def back_idle(carry):
            return jnp.zeros_like(carry[0]), carry[1], carry[2], carry[3]

        def back_step(step, carry):
            active = step == stages - 1 - stage_idx
            grad_next, grad_kept, hidden_kept, dpre_kept = lax.cond(active, back_active, back_idle, carry)
            return lax.ppermute(grad_next, 'stage', to_prev), grad_kept, hidden_kept, dpre_kept

        hidden_init = jnp.zeros((tok_rows, ff_width), jnp.bfloat16)
        _, grad_kept, hidden_kept, dpre_kept = lax.fori_loop(0, stages, back_step, (grad_y, grad_y, hidden_init, hidden_init))
        grad_second = jnp.einsum('nf,nd->fd', hidden_kept, grad_kept, preferred_element_type=jnp.float32)
        grad_first = jnp.einsum('nd,nf->df', x_saved, dpre_kept, preferred_element_type=jnp.float32)

        avg_in = lax.psum(acc_in[0, 0] + grad_first, 'data') / replicas
        avg_out = lax.psum(acc_out[0, 0] + grad_second, 'data') / replicas
        sq_local = jnp.sum(avg_in * avg_in) + jnp.sum(avg_out * avg_out)
        sq_norm = lax.psum(sq_local, 'stage')
        clip_factor = jnp.minimum(1.0, max_norm / (jnp.sqrt(sq_norm) + CLIP_EPS))
        learn_rate = LR_GAIN * w_first.shape[0] ** -0.5
        new_in, mom_in_new, sq_in_new = adamw_update(w_in[0], mom_in[0], sq_in[0], clip_factor * avg_in, learn_rate)
        new_out, mom_out_new, sq_out_new = adamw_update(w_out[0], mom_out[0], sq_out[0], clip_factor * avg_out, learn_rate)
        in_bf = new_in.astype(jnp.bfloat16)
        out_bf = new_out.astype(jnp.bfloat16)
        micro_count = x_next.shape[0]

        def fwd_active(x_in):
            return stage_forward(x_in, in_bf, out_bf)

        def fwd_step(step, carry):
            act_cur, out_buf = carry
            micro_idx = step - stage_idx
            active = (micro_idx >= 0) & (micro_idx < micro_count)
            slot = jnp.clip(micro_idx, 0, micro_count - 1)
            first_in = lax.dynamic_index_in_dim(x_next, slot, 0, keepdims=False)
            x_in = jnp.where(stage_idx == 0, first_in, act_cur)
            y_cur = lax.cond(active, fwd_active, jnp.zeros_like, x_in)
            keep_out = active & (stage_idx == stages - 1)
            out_buf = lax.cond(keep_out, lambda buf: lax.dynamic_update_index_in_dim(buf, y_cur[None], slot, 0), lambda buf: buf, out_buf)
            return lax.ppermute(y_cur, 'stage', to_next), out_buf

        _, out_buf = lax.fori_loop(0, stages + micro_count - 1, fwd_step, (jnp.zeros_like(x_next[0]), jnp.zeros_like(x_next)))
        y_next = lax.psum(jnp.where(stage_idx == stages - 1, out_buf, jnp.zeros_like(out_buf)), 'stage')
        return new_in[None], new_out[None], mom_in_new[None], mom_out_new[None], sq_in_new[None], sq_out_new[None], y_next

    in_specs = (weight_spec,) * 6 + (acc_spec, acc_spec, P('stage', 'data', None), P('data', None), P(None, 'data', None), P())
    out_specs = (weight_spec,) * 6 + (P(None, 'data', None),)
    return jax.shard_map(local_step, mesh=mesh, in_specs=in_specs, out_specs=out_specs, check_vma=False)
```

profile of v0, /device:TPU:31, one launch (start us, length us, event | category | flops | bytes accessed | tf_op | source)
XLA Modules:
  0.0 1026.0 jit_solution(8740997651359409842)
XLA Ops:
  8.1 7.0 convert_bitcast_fusion
  16.2 2.6 convert_bitcast_fusion.1
  18.8 9.6 copy.21
  29.2 87.9 %while.40 = (s32[]{:T(128)}, bf16[64,768]{1,0:T(8,128)(2,1)S(1)}, bf16[64,768]{1,0:T(8,128)(2,1)S(1)}, bf16[64,3072]{1,0:T(8,128)(2,1)S(1)}, bf16[64,3072]{1,0:T...) while((s32[]{:T(128)}, bf16[64,768]{1,0:T(8,128)(2,1)S(1)}, ...), condition=%wide.region_3.0_spmd, body=%wide.region_0.0_spmd.sunk | while | flops 910344192 | bytes 36667664 | solution.py:68
  29.2 11.0 %conditional.6 = (bf16[64,768]{1,0:T(8,128)(2,1)S(1)}, bf16[64,768]{1,0:T(8,128)(2,1)S(1)}, bf16[64,3072]{1,0:T(8,128)(2,1)S(1)}, bf16[64,3072]{1,0:T(8,128)(2,1)}) conditional(s32[]{:T(128)} %convert_element_type.77, (bf16[64,768]{1,0:T(8,128)(2,1)S(1)}, bf16[64,3072]{1,0:T(8,128)(2,1)S(1)}, bf16[64,3072]{1,0:T(8,128)(2,1)}) %tuple.104, ...), branch_computations={%region_1.0_spmd, %region_2.0_spmd} | conditional | flops 910344192 | bytes 36274236 | solution.py:64
  29.2 4.0 fusion.36
  33.3 4.5 multiply_convert_fusion
  37.7 2.5 convolution_convert_fusion
  40.3 1.3 collective-permute-start
  42.6 13.3 %collective-permute-start = (bf16[64,768]{1,0:T(8,128)(2,1)S(1)}, bf16[64,768]{1,0:T(8,128)(2,1)S(1)}, u32[]{:S(2)}, u32[]{:S(2)}) collective-permute-start(bf16[64,768]{1,0:T(8,128)(2,1)S(1)} %get-tuple-element.627), channel_id=1, source_target_pairs={{1,0},{2,1},{3,2},{4,3},{5,4},{6,5},{7,6},{9,8},{10,9},{11,10},{12... | collective-permute-start | bytes 294920 | tf_op jit(solution)/shard_map/while/body/eval_jaxpr/ppermute | solution.py:65
  56.8 3.2 collective-permute-start
  61.0 16.0 %collective-permute-start = (bf16[64,768]{1,0:T(8,128)(2,1)S(1)}, bf16[64,768]{1,0:T(8,128)(2,1)S(1)}, u32[]{:S(2)}, u32[]{:S(2)}) collective-permute-start(bf16[64,768]{1,0:T(8,128)(2,1)S(1)} %get-tuple-element.627), channel_id=1, source_target_pairs={{1,0},{2,1},{3,2},{4,3},{5,4},{6,5},{7,6},{9,8},{10,9},{11,10},{12... | collective-permute-start | bytes 294920 | tf_op jit(solution)/shard_map/while/body/eval_jaxpr/ppermute | solution.py:65
  77.9 5.0 collective-permute-start
  83.9 10.2 collective-permute-start
  95.1 5.0 collective-permute-start
  101.0 15.1 %collective-permute-start = (bf16[64,768]{1,0:T(8,128)(2,1)S(1)}, bf16[64,768]{1,0:T(8,128)(2,1)S(1)}, u32[]{:S(2)}, u32[]{:S(2)}) collective-permute-start(bf16[64,768]{1,0:T(8,128)(2,1)S(1)} %get-tuple-element.627), channel_id=1, source_target_pairs={{1,0},{2,1},{3,2},{4,3},{5,4},{6,5},{7,6},{9,8},{10,9},{11,10},{12... | collective-permute-start | bytes 294920 | tf_op jit(solution)/shard_map/while/body/eval_jaxpr/ppermute | solution.py:65
  117.1 9.1 bitcast_add_fusion.2
  126.2 5.2 bitcast_add_fusion.1
  131.5 9.6 copy.19
  141.7 9.6 copy.20
  151.3 635.3 %all-reduce.6.cloned.1.call-done = (f32[768,3072]{0,1:T(8,128)}, f32[3072,768]{1,0:T(8,128)}) async-done(((f32[768,3072]{0,1:T(8,128)}, f32[3072,768]{1,0:T(8,128)}), (f32[768,3072]{0,1:T(8,128)}, f32[3072,768]{1,0:T(8,128)})) %all-reduce.6.cloned.1.call-update) | async-done | bytes 18874384 | tf_op jit(solution)/shard_map/psum | solution.py:72
  786.6 6.9 multiply_reduce_fusion
  793.4 3.0 multiply_reduce_fusion.1
  797.8 9.6 copy.22
  807.3 11.9 %psum.30 = f32[]{:T(128)} all-reduce(f32[]{:T(128)S(6)} %add.104), channel_id=1, replica_groups=mesh['data'=4,'stage'=8] {'stage'}, use_global_device_ids=true, to_apply=%region_8.0 | all-reduce | flops 1 | bytes 8 | tf_op jit(solution)/shard_map/psum | solution.py:75
  820.0 28.2 %fusion.35 = (bf16[768,3072]{0,1:T(8,128)(2,1)}, f32[768,3072]{0,1:T(8,128)}, f32[1,768,3072]{1,2,0:T(8,128)}, f32[1,768,3072]{1,2,0:T(8,128)}) fusion(f32[1,768,3072]{1,2,0:T(8,128)} %copy.22, f32[768,3072]{0,1:T(8,128)} %get-tuple-element.510, f32[]{:T(128)S(6)} %mul.180, f32[1,768,3072]{1,2,0:T(8,128)} %copy.20, f32[1,768,3072]{1,2,0:T(8,128)} %copy.19), kind=kLoop, calls=%fused_computation.53 | loop fusion | flops 35389440 | bytes 70778880 | tf_op jit(solution)/shard_map/convert_element_type | solution.py:80
  848.2 6.6 copy.23
  854.9 28.2 %fusion.34 = (bf16[3072,768]{1,0:T(8,128)(2,1)}, f32[3072,768]{1,0:T(8,128)}, f32[1,3072,768]{2,1,0:T(8,128)}, f32[1,3072,768]{2,1,0:T(8,128)}) fusion(f32[1,3072,768]{2,1,0:T(8,128)} %param.27, f32[3072,768]{1,0:T(8,128)} %get-tuple-element.511, f32[]{:T(128)S(6)} %mul.180, f32[1,3072,768]{2,1,0:T(8,128)} %param.25, f32[1,3072,768]{2,1,0:T(8,128)} %param.23), kind=kLoop, calls=%fused_computation.52 | loop fusion | flops 35389440 | bytes 70778880 | tf_op jit(solution)/shard_map/convert_element_type | solution.py:81
  883.1 82.4 %while.41 = (s32[]{:T(128)}, bf16[64,768]{1,0:T(8,128)(2,1)S(1)}, bf16[1,64,768]{2,1,0:T(8,128)(2,1)S(1)}, s32[]{:T(128)}, pred[]{:T(512)}, /*index=5*/bf16[1,64...) while((s32[]{:T(128)}, bf16[64,768]{1,0:T(8,128)(2,1)S(1)}, ...), condition=%wide.region_14.15_spmd, body=%wide.region_9.14_spmd.sunk | while | flops 605847552 | bytes 10322172 | solution.py:99
  883.8 1.3 collective-permute-start.1
  885.1 1.9 collective-permute-done.1
  887.7 1.3 collective-permute-start.1
  889.0 3.6 collective-permute-done.1
  893.2 1.3 collective-permute-start.1
  894.6 4.6 collective-permute-done.1
  899.8 1.3 collective-permute-start.1
  901.1 4.6 collective-permute-done.1
  906.4 1.3 collective-permute-start.1
  907.7 4.7 collective-permute-done.1
  914.4 5.5 collective-permute-done.1
  921.8 34.2 %collective-permute-done.1 = bf16[64,768]{1,0:T(8,128)(2,1)S(1)} collective-permute-done((bf16[64,768]{1,0:T(8,128)(2,1)}, bf16[64,768]{1,0:T(8,128)(2,1)S(1)}, u32[]{:S(2)}, u32[]{:S(2)}) %collective-permute-start.1) | collective-permute-done | bytes 98336 | tf_op jit(solution)/shard_map/while/body/eval_jaxpr/ppermute | solution.py:97
  956.1 6.3 conditional.7
  956.1 6.3 convolution_convert_fusion.1
  966.2 9.6 copy.24
  975.8 9.6 copy.25
  985.4 9.6 copy.26
  995.0 22.6 %all-reduce.4.cloned.1.call-done = bf16[1,64,768]{2,1,0:T(8,128)(2,1)} async-done(((bf16[1,64,768]{2,1,0:T(8,128)(2,1)}), bf16[1,64,768]{2,1,0:T(8,128)(2,1)}) %all-reduce.4.cloned.1.call-update) | async-done | bytes 98320 | tf_op jit(solution)/shard_map/psum | solution.py:100
  1017.6 1.5 copy.69
  (73 shorter events, 27.0 us)
Async XLA Ops:
  7.2 779.4 %all-reduce.6.cloned.1.call-start = ((), (), s32[]{:S(2)}) async-start(), calls=%async_computation.1 | async-start | bytes 37748736 | tf_op jit(solution)/shard_map/psum | solution.py:72
  8.1 8.1 copy-start.1
  18.8 10.4 %copy-start.5 = (bf16[1,64,768]{2,1,0:T(8,128)(2,1)S(1)}, bf16[1,64,768]{2,1,0:T(8,128)(2,1)}, u32[]{:S(2)}) copy-start(bf16[1,64,768]{2,1,0:T(8,128)(2,1)} %param.30) | copy-start | bytes 294916
  29.2 8.5 copy-start
  40.3 2.2 collective-permute-start
  42.6 14.2 %collective-permute-start = (bf16[64,768]{1,0:T(8,128)(2,1)S(1)}, bf16[64,768]{1,0:T(8,128)(2,1)S(1)}, u32[]{:S(2)}, u32[]{:S(2)}) collective-permute-start(bf16[64,768]{1,0:T(8,128)(2,1)S(1)} %get-tuple-element.627), channel_id=1, source_target_pairs={{1,0},{2,1},{3,2},{4,3},{5,4},{6,5},{7,6},{9,8},{10,9},{11,10},{12... | collective-permute-start | bytes 294920 | tf_op jit(solution)/shard_map/while/body/eval_jaxpr/ppermute | solution.py:65
  56.8 4.1 collective-permute-start
  61.0 17.0 %collective-permute-start = (bf16[64,768]{1,0:T(8,128)(2,1)S(1)}, bf16[64,768]{1,0:T(8,128)(2,1)S(1)}, u32[]{:S(2)}, u32[]{:S(2)}) collective-permute-start(bf16[64,768]{1,0:T(8,128)(2,1)S(1)} %get-tuple-element.627), channel_id=1, source_target_pairs={{1,0},{2,1},{3,2},{4,3},{5,4},{6,5},{7,6},{9,8},{10,9},{11,10},{12... | collective-permute-start | bytes 294920 | tf_op jit(solution)/shard_map/while/body/eval_jaxpr/ppermute | solution.py:65
  77.9 5.9 collective-permute-start
  83.9 11.1 %collective-permute-start = (bf16[64,768]{1,0:T(8,128)(2,1)S(1)}, bf16[64,768]{1,0:T(8,128)(2,1)S(1)}, u32[]{:S(2)}, u32[]{:S(2)}) collective-permute-start(bf16[64,768]{1,0:T(8,128)(2,1)S(1)} %get-tuple-element.627), channel_id=1, source_target_pairs={{1,0},{2,1},{3,2},{4,3},{5,4},{6,5},{7,6},{9,8},{10,9},{11,10},{12... | collective-permute-start | bytes 294920 | tf_op jit(solution)/shard_map/while/body/eval_jaxpr/ppermute | solution.py:65
  95.1 5.9 collective-permute-start
  101.0 16.0 %collective-permute-start = (bf16[64,768]{1,0:T(8,128)(2,1)S(1)}, bf16[64,768]{1,0:T(8,128)(2,1)S(1)}, u32[]{:S(2)}, u32[]{:S(2)}) collective-permute-start(bf16[64,768]{1,0:T(8,128)(2,1)S(1)} %get-tuple-element.627), channel_id=1, source_target_pairs={{1,0},{2,1},{3,2},{4,3},{5,4},{6,5},{7,6},{9,8},{10,9},{11,10},{12... | collective-permute-start | bytes 294920 | tf_op jit(solution)/shard_map/while/body/eval_jaxpr/ppermute | solution.py:65
  117.1 9.1 copy-start.3
  131.4 886.2 %all-reduce.4.cloned.1.call-start = ((), (), s32[]{:S(2)}) async-start(), calls=%async_computation | async-start | bytes 196608 | tf_op jit(solution)/shard_map/psum | solution.py:100
  786.6 6.9 copy-start.2
  854.8 28.3 %copy-start.4 = (bf16[1,64,768]{2,1,0:T(8,128)(2,1)S(1)}, bf16[1,64,768]{2,1,0:T(8,128)(2,1)}, u32[]{:S(2)}) copy-start(bf16[1,64,768]{2,1,0:T(8,128)(2,1)} %param.32) | copy-start | bytes 294916
  883.8 3.2 collective-permute-start.1
  887.7 4.9 collective-permute-start.1
  893.2 5.9 collective-permute-start.1
  899.8 5.9 collective-permute-start.1
  906.4 6.0 collective-permute-start.1
  913.1 6.8 collective-permute-start.1
  920.5 35.5 %collective-permute-start.1 = (bf16[64,768]{1,0:T(8,128)(2,1)}, bf16[64,768]{1,0:T(8,128)(2,1)S(1)}, u32[]{:S(2)}, u32[]{:S(2)}) collective-permute-start(bf16[64,768]{1,0:T(8,128)(2,1)} %get-tuple-element.720), channel_id=1, source_target_pairs={{0,1},{1,2},{2,3},{3,4},{4,5},{5,6},{6,7},{8,9},{9,10},{10,11},{11... | collective-permute-start | bytes 294920 | tf_op jit(solution)/shard_map/while/body/eval_jaxpr/ppermute | solution.py:97
  962.4 3.2 collective-permute-start.1
Sparse Core Ops, SparseCore 0:
  131.5 654.9 all-reduce.5
  966.4 51.1 all-reduce.3
where the time goes:
time: 1030 us
  waiting for transfers between devices  725 us (70%)
  local copies, waits for them, and re-layouts  83.6 us (8%)
  starting transfers between devices  79.5 us (8%)
  other arithmetic  76.6 us (7%)
  matrix products  31.6 us (3%)
  between operations  16.8 us (2%)
  blocking collectives  11.9 us (1%)
    psum x1, waiting for transfers between devices, local_step(): avg_in = lax.psum(acc_in[0, 0] + grad_first, 'data') / replicas  635 us
    unnamed x20, local copies, waits for them, and re-layouts  70.7 us
    ppermute x8, starting transfers between devices, back_step(): lax.ppermute(grad_next, 'stage', to_prev)  69.2 us
    ppermute x8, waiting for transfers between devices, fwd_step(): return (lax.ppermute(y_cur, 'stage', to_next), out_buf)  60.1 us
    convert_element_type x1, other arithmetic, local_step(): out_bf = new_out.astype(jnp.bfloat16)  28.2 us
    convert_element_type x1, other arithmetic, local_step(): in_bf = new_in.astype(jnp.bfloat16)  28.2 us
    psum x1, waiting for transfers between devices, local_step(): lax.psum(jnp.where(stage_idx == stages - 1, out_buf, jnp.zeros_like(out_b...  22.6 us
  transfers between devices with their start and end apart: 18, of which 18 were waited for; matrix products, arithmetic and copies ran while one was open for 5% of the time, Pallas kernels for 0%

commit v1 on v0

v1 whole, which is shorter than its diff:
```python
import math

import jax
import jax.numpy as jnp
from jax import lax
from jax.experimental import pallas as pl
from jax.experimental.pallas import tpu as pltpu
from jax.sharding import PartitionSpec as P

BETA_ONE = 0.9
BETA_TWO = 0.95
ADAM_EPS = 1e-8
WEIGHT_DECAY = 0.1
LR_GAIN = 0.2
CLIP_EPS = 1e-6
STEP_COUNT = 20
MESH = pl.DeviceIdType.MESH
F32, BF16 = jnp.float32, jnp.bfloat16

D, FF, STAGES, REPLICAS, TOK = 768, 3072, 8, 4, 64
ROWS = REPLICAS * TOK
CHUNKS = 24
R1, R2 = D // CHUNKS, FF // CHUNKS
TILE = 256
SLOTS = 8
EARLY = 4
LEARN_RATE = LR_GAIN * D ** -0.5
GELU_K = math.sqrt(2.0 / math.pi)
NT = (((1,), (1,)), ((), ()))
TN = (((0,), (0,)), ((), ()))
NN = (((1,), (0,)), ((), ()))


def mm(lhs, rhs, dims):
    return lax.dot_general(lhs, rhs, dims, preferred_element_type=F32)


def gelu_parts(z):
    zz = z * z
    tanh = jnp.tanh(GELU_K * (z + 0.044715 * (zz * z)))
    cdf = 0.5 * (1.0 + tanh)
    slope = cdf + (0.5 * z) * (1.0 - tanh * tanh) * (GELU_K * (1.0 + (3 * 0.044715) * zz))
    return z * cdf, slope


def gelu(z):
    return z * (0.5 * (1.0 + jnp.tanh(GELU_K * (z + 0.044715 * (z * z * z)))))


def clip_of(sq_norm, max_norm):
    return jnp.minimum(1.0, max_norm / (jnp.sqrt(sq_norm) + CLIP_EPS))


def adamw(weight, moment, sq_moment, gradient):
    moment_new = BETA_ONE * moment + (1.0 - BETA_ONE) * gradient
    sq_new = BETA_TWO * sq_moment + (1.0 - BETA_TWO) * gradient * gradient
    m_hat = moment_new / (1.0 - BETA_ONE ** STEP_COUNT)
    v_hat = sq_new / (1.0 - BETA_TWO ** STEP_COUNT)
    weight_new = weight * (1.0 - LEARN_RATE * WEIGHT_DECAY) - LEARN_RATE * m_hat / (jnp.sqrt(v_hat) + ADAM_EPS)
    return weight_new, moment_new, sq_new


def owner_of(stage):
    return 3 * ((stage % 2 + (stage // 2) % 2) % 2)


def ds(index, size):
    return pl.ds(pl.multiple_of(index * size, size), size)


def step_kernel(w1, w2, m1, m2, v1, v2, acc1, acc2, a_in, gy_in, x_in, maxn,
                g1_o, g2_o, nrm_o, y_o,
                recv1, recv2, own1, own2, b1, b2, gp, hid, dz, abuf, gbuf, gnext, xbuf, ybuf, sq1, sq2, nbuf, nres,
                a_snd, a_rcv, in_snd, in_rcv, g_snd, g_rcv, x_snd, x_rcv, y_snd, y_rcv, rs_snd, rs_rcv, ag_snd, ag_rcv,
                n_snd, n_rcv, nt_snd, nt_rcv, ld, st, loc):
    r = lax.axis_index("data")
    s = lax.axis_index("stage")
    own_r = owner_of(s)
    away = 1 - 2 * (own_r // 3)
    d = (r - own_r) * away
    accs, recvs, owns, gouts = (acc1, acc2), (recv1, recv2), (own1, own2), (g1_o, g2_o)
    heights = (R1, R2)

    def remote(src, dst, snd, rcv, to_r, to_s):
        return pltpu.make_async_remote_copy(src_ref=src, dst_ref=dst, send_sem=snd, recv_sem=rcv,
                                            device_id=(to_r, to_s), device_id_type=MESH)

    def arrive(ref, sem):
        pltpu.make_async_copy(ref, ref, sem).wait()

    def gather(src, dst, snd, rcv):
        part = dst.at[ds(r, TOK), :]

        @pl.when(d == 0)
        def _():
            pltpu.make_async_copy(src, part, rcv.at[r]).start()

        @pl.when(d != 0)
        def _():
            remote(src, part, snd, rcv.at[r], own_r, s).start()

    def gathered(dst, rcv):
        for q in range(REPLICAS):
            arrive(dst.at[pl.ds(q * TOK, TOK), :], rcv.at[q])

    @pl.when(s == STAGES - 1)
    def _():
        gather(gy_in, gbuf, in_snd, in_rcv)

    gather(a_in, abuf, a_snd, a_rcv)

    @pl.when(s == 0)
    def _():
        gather(x_in, xbuf, in_snd, in_rcv)

    def rs_copy(mat, k, src):
        part = recvs[mat].at[ds(k, heights[mat]), :]
        sem = mat * CHUNKS + k
        return remote(src, part, rs_snd.at[sem], rs_rcv.at[sem], r - away, s)

    def rs_src(mat, k):
        return accs[mat].at[0, 0, ds(k, heights[mat]), :]

    def ag_copy(mat, k, from_vmem):
        rows = ds(k, heights[mat])
        src = recvs[mat] if from_vmem else gouts[mat]
        sem = mat * CHUNKS + k
        return remote(src.at[rows, :], gouts[mat].at[rows, :], ag_snd.at[sem], ag_rcv.at[sem], r + away, s)

    def each(mats, fn, lo=0, hi=CHUNKS):
        for mat in mats:
            @pl.loop(lo, hi)
            def _(k):
                fn(mat, k)

    @pl.when(d == 3)
    def _():
        each((0, 1), lambda mat, k: rs_copy(mat, k, rs_src(mat, k)).start())

    @pl.when((d == 1) | (d == 2))
    def _():
        own_copies = [pltpu.make_async_copy(accs[mat].at[0, 0], owns[mat], ld.at[mat, 0]) for mat in (0, 1)]
        for copy in own_copies:
            copy.start()
        for mat in (0, 1):
            own_copies[mat].wait()

            @pl.loop(0, CHUNKS)
            def _(k):
                rows = ds(k, heights[mat])
                arrive(recvs[mat].at[rows, :], rs_rcv.at[mat * CHUNKS + k])
                recvs[mat][rows, :] = recvs[mat][rows, :] + owns[mat][rows, :]
                rs_copy(mat, k, recvs[mat].at[rows, :]).start()

    @pl.when(d != 0)
    def _():
        for mat in (0, 1):
            @pl.loop(0, CHUNKS)
            def _(k):
                rows = ds(k, heights[mat])
                arrive(gouts[mat].at[rows, :], ag_rcv.at[mat * CHUNKS + k])

                @pl.when(d != 3)
                def _():
                    ag_copy(mat, k, False).start()

                if mat == 1:
                    @pl.when((s == STAGES - 1) & (k == CHUNKS - 8))
                    def _():
                        arrive(y_o, y_rcv)
                        for t in range(1, STAGES):
                            remote(y_o, y_o, y_snd.at[t], y_rcv, r, (s + t) % STAGES).start()

        arrive(nres, nt_rcv)
        remote(a_in, abuf.at[ds(r, TOK), :], a_snd, a_rcv.at[r], own_r, s).wait_send()

        @pl.when((s == 0) | (s == STAGES - 1))
        def _():
            remote(x_in, xbuf.at[ds(r, TOK), :], in_snd, in_rcv.at[r], own_r, s).wait_send()

        each((0, 1), lambda mat, k: rs_copy(mat, k, rs_src(mat, k)).wait_send())

        @pl.when(d != 3)
        def _():
            each((0, 1), lambda mat, k: ag_copy(mat, k, False).wait_send())

    @pl.when(d == 0)
    def _():
        loads = [pltpu.make_async_copy(w.at[0], own, ld.at[mat, 0]) for mat, (w, own) in enumerate(((w1, own1), (w2, own2)))]
        for copy in loads:
            copy.start()
        sq1[...] = jnp.zeros_like(sq1)
        sq2[...] = jnp.zeros_like(sq2)
        loads[0].wait()

        @pl.loop(0, CHUNKS)
        def _(k):
            b1[ds(k, R1), :] = own1[ds(k, R1), :].astype(BF16)

        loads[1].wait()

        @pl.loop(0, CHUNKS)
        def _(k):
            b2[ds(k, R2), :] = own2[ds(k, R2), :].astype(BF16)

        own_copies = [pltpu.make_async_copy(accs[mat].at[0, 0], owns[mat], ld.at[mat, 1]) for mat in (0, 1)]
        for copy in own_copies:
            copy.start()

        gathered(abuf, a_rcv)

        @pl.loop(0, FF // TILE)
        def _(j):
            cols = ds(j, TILE)
            value, slope = gelu_parts(mm(abuf[...], b1[:, cols], NN))
            hid[:, cols] = value.astype(BF16)
            gp[:, cols] = slope

        @pl.when(s == STAGES - 1)
        def _():
            gathered(gbuf, in_rcv)

        @pl.when(s != STAGES - 1)
        def _():
            arrive(gbuf, g_rcv)

        @pl.loop(0, FF // TILE)
        def _(j):
            cols = ds(j, TILE)
            dz[:, cols] = (gp[:, cols] * mm(gbuf[...], b2[cols, :], NT)).astype(BF16)

        send_g = remote(gnext, gbuf, g_snd, g_rcv, owner_of(s + STAGES - 1), (s + STAGES - 1) % STAGES)

        @pl.when(s != 0)
        def _():
            @pl.loop(0, D // TILE)
            def _(j):
                gnext[:, ds(j, TILE)] = mm(dz[...], b1[ds(j, TILE), :], NT).astype(BF16)

            send_g.start()

        own_copies[0].wait()

        @pl.loop(0, FF // TILE)
        def _(j):
            cols = ds(j, TILE)
            own1[:, cols] = own1[:, cols] + mm(abuf[...], dz[:, cols], TN)

        own_copies[1].wait()

        @pl.loop(0, FF // TILE)
        def _(j):
            cols = ds(j, TILE)
            own2[cols, :] = own2[cols, :] + mm(hid[:, cols], gbuf[...], TN)

        for mat in (0, 1):
            sq = (sq1, sq2)[mat]

            @pl.loop(0, CHUNKS)
            def _(k):
                rows = ds(k, heights[mat])
                arrive(recvs[mat].at[rows, :], rs_rcv.at[mat * CHUNKS + k])
                avg = (recvs[mat][rows, :] + owns[mat][rows, :]) * (1.0 / REPLICAS)
                recvs[mat][rows, :] = avg
                part = avg[0:8, :] * avg[0:8, :]
                for i in range(1, heights[mat] // 8):
                    part = part + avg[8 * i:8 * i + 8, :] * avg[8 * i:8 * i + 8, :]
                sq[...] = sq[...] + part
                if mat == 1:
                    @pl.when(k >= CHUNKS - EARLY)
                    def _():
                        ag_copy(0, k - (CHUNKS - EARLY), True).start()

        partial = jnp.sum(sq1[...], keepdims=True) + jnp.sum(sq2[...], keepdims=True)
        nbuf[s] = jnp.broadcast_to(partial, (8, 128))
        norm_copies = []
        for t in range(1, STAGES):
            peer = (s + t) % STAGES
            norm_copies.append(remote(nbuf.at[s], nbuf.at[s], n_snd.at[t], n_rcv.at[s], owner_of(peer), peer))
            norm_copies[-1].start()
        for t in range(1, STAGES):
            peer = (s + t) % STAGES
            arrive(nbuf.at[peer], n_rcv.at[peer])
        total = nbuf[0]
        for t in range(1, STAGES):
            total = total + nbuf[t]
        nres[...] = total
        total_copies = [remote(nres, nres, nt_snd.at[q], nt_rcv, own_r + q * away, s) for q in range(1, REPLICAS)]
        for copy in total_copies:
            copy.start()

        chained = (s % 2 == 0) | (s == STAGES - 1)
        first = jnp.where(chained, 8 + 2 * s, CHUNKS)

        @pl.loop(EARLY, first)
        def _(k):
            ag_copy(0, k, True).start()

        @pl.when(jnp.logical_not(chained))
        def _():
            @pl.loop(0, CHUNKS)
            def _(k):
                ag_copy(1, k, True).start()

        local_copies = [pltpu.make_async_copy(recvs[mat], gouts[mat], loc.at[mat]) for mat in (0, 1)]
        for copy in local_copies:
            copy.start()

        clip = clip_of(total, maxn[...])[0:1, 0:1]
        for mat, (weights, hbm) in enumerate(((b1, (w1, m1, v1)), (b2, (w2, m2, v2)))):
            height = heights[mat]

            def fetch(k, i):
                slot = (k % SLOTS) * 3 + i
                return pltpu.make_async_copy(hbm[i].at[0, ds(k, height), :], owns[mat].at[ds(slot, height), :], st.at[mat, slot])

            for k in range(SLOTS):
                for i in range(3):
                    fetch(k, i).start()

            @pl.loop(0, CHUNKS)
            def _(k):
                for i in range(3):
                    fetch(k, i).wait()
                rows = ds(k, height)
                parts = [owns[mat][ds((k % SLOTS) * 3 + i, height), :] for i in range(3)]
                new_weight, _, _ = adamw(*parts, clip * recvs[mat][rows, :])
                weights[rows, :] = new_weight.astype(BF16)

                @pl.when(k + SLOTS < CHUNKS)
                def _():
                    for i in range(3):
                        fetch(k + SLOTS, i).start()

        @pl.when(s == 0)
        def _():
            gathered(xbuf, in_rcv)

        @pl.when(s != 0)
        def _():
            arrive(xbuf, x_rcv)

        @pl.loop(0, FF // TILE)
        def _(j):
            cols = ds(j, TILE)
            hid[:, cols] = gelu(mm(xbuf[...], b1[:, cols], NN)).astype(BF16)

        @pl.loop(0, D // TILE)
        def _(j):
            ybuf[:, ds(j, TILE)] = mm(hid[...], b2[:, ds(j, TILE)], NN).astype(BF16)

        send_x = remote(ybuf, xbuf, x_snd, x_rcv, owner_of(s + 1), (s + 1) % STAGES)

        @pl.when(s != STAGES - 1)
        def _():
            send_x.start()

        y_rows = ybuf.at[ds(r, TOK), :]

        @pl.when(s == STAGES - 1)
        def _():
            keep = pltpu.make_async_copy(y_rows, y_o, loc.at[2])
            keep.start()
            for q in range(1, REPLICAS):
                remote(ybuf.at[ds(own_r + q * away, TOK), :], y_o, y_snd.at[q + STAGES], y_rcv, own_r + q * away, s).start()
            keep.wait()
            for t in range(1, STAGES):
                remote(y_o, y_o, y_snd.at[t], y_rcv, r, (s + t) % STAGES).start()

        @pl.when(chained)
        def _():
            @pl.loop(first, CHUNKS)
            def _(k):
                ag_copy(0, k, True).start()

            @pl.loop(0, CHUNKS)
            def _(k):
                ag_copy(1, k, True).start()

        @pl.when(s == STAGES - 1)
        def _():
            for q in range(1, REPLICAS):
                remote(ybuf.at[ds(own_r + q * away, TOK), :], y_o, y_snd.at[q + STAGES], y_rcv, own_r + q * away, s).wait_send()

        @pl.when(s != 0)
        def _():
            send_g.wait_send()

        @pl.when(s != STAGES - 1)
        def _():
            send_x.wait_send()

        for copy in norm_copies + total_copies:
            copy.wait_send()
        for copy in local_copies:
            copy.wait()
        each((0, 1), lambda mat, k: ag_copy(mat, k, True).wait_send())

    nrm_o[...] = nres[...]

    @pl.when(s != STAGES - 1)
    def _():
        arrive(y_o, y_rcv)

    @pl.when(s == STAGES - 1)
    def _():
        for t in range(1, STAGES):
            remote(y_o, y_o, y_snd.at[t], y_rcv, r, (s + t) % STAGES).wait_send()


def update_kernel(nrm, maxn, *refs):
    clip = clip_of(nrm[...], maxn[...])[0:1, 0:1]
    for mat in (0, 1):
        weight, moment, sq_moment, grad = (ref[...] for ref in refs[4 * mat:4 * mat + 4])
        new = adamw(weight[0], moment[0], sq_moment[0], clip * grad)
        for ref, value in zip(refs[8 + 3 * mat:11 + 3 * mat], new):
            ref[0] = value


def solution(mesh):
    assert mesh.shape["stage"] == STAGES and mesh.shape["data"] == REPLICAS
    weight_spec = P("stage", None, None)
    acc_spec = P("data", "stage", None, None)

    def local_step(w_in, w_out, mom_in, mom_out, sq_in, sq_out, acc_in, acc_out, stage_acts, grad_y, x_next, max_norm):
        maxn = jnp.full((8, 128), max_norm, F32)
        hbm = pl.BlockSpec(memory_space=pl.ANY)
        vmem = pl.BlockSpec(memory_space=pltpu.VMEM)
        dma = pltpu.SemaphoreType.DMA
        g1, g2, nrm, y = pl.pallas_call(
            step_kernel,
            out_shape=(
                jax.ShapeDtypeStruct((D, FF), F32), jax.ShapeDtypeStruct((FF, D), F32),
                jax.ShapeDtypeStruct((8, 128), F32), jax.ShapeDtypeStruct((TOK, D), BF16),
            ),
            in_specs=[hbm] * 11 + [vmem],
            out_specs=(hbm, hbm, vmem, hbm),
            scratch_shapes=[
                pltpu.VMEM((D, FF), F32), pltpu.VMEM((FF, D), F32),
                pltpu.VMEM((D, FF), F32), pltpu.VMEM((FF, D), F32),
                pltpu.VMEM((D, FF), BF16), pltpu.VMEM((FF, D), BF16),
                pltpu.VMEM((ROWS, FF), F32), pltpu.VMEM((ROWS, FF), BF16), pltpu.VMEM((ROWS, FF), BF16),
                pltpu.VMEM((ROWS, D), BF16), pltpu.VMEM((ROWS, D), BF16), pltpu.VMEM((ROWS, D), BF16),
                pltpu.VMEM((ROWS, D), BF16), pltpu.VMEM((ROWS, D), BF16),
                pltpu.VMEM((8, FF), F32), pltpu.VMEM((8, D), F32),
                pltpu.VMEM((STAGES, 8, 128), F32), pltpu.VMEM((8, 128), F32),
                dma, dma((REPLICAS,)), dma, dma((REPLICAS,)), dma, dma, dma, dma, dma((STAGES + REPLICAS,)), dma,
                dma((2 * CHUNKS,)), dma((2 * CHUNKS,)), dma((2 * CHUNKS,)), dma((2 * CHUNKS,)),
                dma((STAGES,)), dma((STAGES,)), dma((REPLICAS,)), dma,
                dma((2, 2)), dma((2, 3 * SLOTS)), dma((3,)),
            ],
            compiler_params=pltpu.CompilerParams(has_side_effects=True, vmem_limit_bytes=67043328),
            name="reduce_backward_broadcast_forward",
        )(w_in, w_out, mom_in, mom_out, sq_in, sq_out, acc_in, acc_out, stage_acts[0], grad_y, x_next[0], maxn)

        one = pl.BlockSpec((8, 128), lambda k: (0, 0))
        wide = pl.BlockSpec((1, R1, FF), lambda k: (0, k, 0))
        tall = pl.BlockSpec((1, R2, D), lambda k: (0, k, 0))
        new = pl.pallas_call(
            update_kernel,
            grid=(CHUNKS,),
            out_shape=[jax.ShapeDtypeStruct((1, D, FF), F32)] * 3 + [jax.ShapeDtypeStruct((1, FF, D), F32)] * 3,
            in_specs=[one, one] + [wide] * 3 + [pl.BlockSpec((R1, FF), lambda k: (k, 0))] + [tall] * 3 + [pl.BlockSpec((R2, D), lambda k: (k, 0))],
            out_specs=[wide] * 3 + [tall] * 3,
            name="adamw_update",
        )(nrm, maxn, w_in, mom_in, sq_in, g1, w_out, mom_out, sq_out, g2)
        return new[0], new[3], new[1], new[4], new[2], new[5], y[None]

    in_specs = (weight_spec,) * 6 + (acc_spec, acc_spec, P("stage", "data", None), P("data", None), P(None, "data", None), P())
    out_specs = (weight_spec,) * 6 + (P(None, "data", None),)
    return jax.shard_map(local_step, mesh=mesh, in_specs=in_specs, out_specs=out_specs, check_vma=False)
```

time: 1030 us -> 553 us (0.54)
  waiting for transfers between devices: 725 us -> 0 us
  Pallas kernels: 0 us -> 551 us
  local copies, waits for them, and re-layouts: 83.6 us -> 1.24 us
  starting transfers between devices: 79.5 us -> 0 us
  other arithmetic: 76.6 us -> 0 us
  matrix products: 31.6 us -> 0 us
  between operations: 16.8 us -> 1.31 us
  blocking collectives: 11.9 us -> 0 us
    psum x2 -> x0, waiting for transfers between devices: 658 us -> none  [the longest x1 635 us: local_step(): avg_in = lax.psum(acc_in[0, 0] + grad_first, 'data') / replicas]
    pallas_call x0 -> x2, Pallas kernels: none -> 551 us  [the longest x1 500 us: local_step(): pl.pallas_call(step_kernel, out_shape=(jax.ShapeDtypeStruct((D, FF), F32)...]
    ppermute x16 -> x0, starting transfers between devices: 79.4 us -> none  [the longest x8 69.2 us: back_step(): lax.ppermute(grad_next, 'stage', to_prev)]
    unnamed x20 -> x3, local copies, waits for them, and re-layouts: 70.7 us -> 0.65 us
    ppermute x16 -> x0, waiting for transfers between devices: 67.5 us -> none  [the longest x8 60.1 us: fwd_step(): return (lax.ppermute(y_cur, 'stage', to_next), out_buf)]
    convert_element_type x4 -> x0, other arithmetic: 66.1 us -> none  [the longest x1 28.2 us: local_step(): out_bf = new_out.astype(jnp.bfloat16)]
    dot_general x6 -> x0, matrix products: 31.6 us -> none  [the longest x1 9.12 us: local_step(): jnp.einsum('nd,nf->df', x_saved, dpre_kept, preferred_element_type=jnp.fl...]
    psum x1 -> x0, blocking collectives: 11.9 us -> none  [local_step(): sq_norm = lax.psum(sq_local, 'stage')]
  transfers between devices with their start and end apart: 18 -> 0, of which waited for: 18 -> 0; matrix products, arithmetic and copies ran while one was open for 5% -> 0% of each run, Pallas kernels for 0% -> 0%
where the time goes in v1:
time: 553 us
  Pallas kernels  551 us (100%)
    pallas_call x1, Pallas kernels, local_step(): pl.pallas_call(step_kernel, out_shape=(jax.ShapeDtypeStruct((D, FF), F32)...  500 us
    pallas_call x1, Pallas kernels, local_step(): pl.pallas_call(update_kernel, grid=(CHUNKS,), out_shape=[jax.ShapeDtypeSt...  50.7 us

profile of v1, /device:TPU:31, one launch (start us, length us, event | category | flops | bytes accessed | tf_op | source)
XLA Modules:
  0.0 553.3 jit_solution(13709711383677504998)
XLA Ops:
  1.3 0.6 broadcast_in_dim.6.maxn
  1.9 500.1 %reduce_backward_broadcast_forward.1 = (f32[768,3072]{1,0:T(8,128)}, f32[3072,768]{1,0:T(8,128)}, f32[8,128]{1,0:T(8,128)}, bf16[64,768]{1,0:T(8,128)(2,1)}) custom-call(f32[1,768,3072]{2,1,0:T(8,128)} %refs_0_.1, f32[1,3072,768]{2,1,0:T(8,128)} %refs_4_.1, f32[1,768,3072]{2,1,0:T(8,128)} %refs_1_.1, f32[1,3072,768]{2,1,0:T(8,128)} %refs_5_.1, ...), custom_call_target="tpu_custom_call" | custom-call | tf_op jit(solution)/shard_map/reduce_backward_broadcast_forward/pallas_call | solution.py:430
  501.9 0.0 copy-start
  502.0 50.7 %adamw_update.1 = (f32[1,768,3072]{2,1,0:T(8,128)}, f32[1,768,3072]{2,1,0:T(8,128)}, f32[1,768,3072]{2,1,0:T(8,128)}, f32[1,3072,768]{2,1,0:T(8,128)}, f32[1,3072,768]{2,1,0:T(8,128)}, /*index=5*/f32[1,3072,768]{2,1,0:T(8,128)}) custom-call(f32[8,128]{1,0:T(8,128)} %get-tuple-element.17.nrm, f32[8,128]{1,0:T(8,128)} %broadcast_in_dim.6.maxn, ...), custom_call_target="tpu_custom_call" | custom-call | tf_op jit(solution)/shard_map/adamw_update/pallas_call | solution.py:459
  552.6 0.0 copy-done
  552.6 0.6 copy.21
Async XLA Ops:
  501.9 50.7 %copy-start = (bf16[64,768]{1,0:T(8,128)(2,1)S(1)}, bf16[64,768]{1,0:T(8,128)(2,1)}, u32[]{:S(2)}) copy-start(bf16[64,768]{1,0:T(8,128)(2,1)} %get-tuple-element.26) | copy-start | bytes 294916

commit v2 on v1

--- a/solution.py
+++ b/solution.py
@@ -19,11 +19,12 @@
 
 D, FF, STAGES, REPLICAS, TOK = 768, 3072, 8, 4, 64
 ROWS = REPLICAS * TOK
-CHUNKS = 24
+CHUNKS = 48
 R1, R2 = D // CHUNKS, FF // CHUNKS
+UPDATES = 16
 TILE = 256
-SLOTS = 8
-EARLY = 4
+SLOTS = 16
+EARLY = (16, 2)
 LEARN_RATE = LR_GAIN * D ** -0.5
 GELU_K = math.sqrt(2.0 / math.pi)
 NT = (((1,), (1,)), ((), ()))
@@ -54,9 +55,9 @@
 def adamw(weight, moment, sq_moment, gradient):
     moment_new = BETA_ONE * moment + (1.0 - BETA_ONE) * gradient
     sq_new = BETA_TWO * sq_moment + (1.0 - BETA_TWO) * gradient * gradient
-    m_hat = moment_new / (1.0 - BETA_ONE ** STEP_COUNT)
-    v_hat = sq_new / (1.0 - BETA_TWO ** STEP_COUNT)
-    weight_new = weight * (1.0 - LEARN_RATE * WEIGHT_DECAY) - LEARN_RATE * m_hat / (jnp.sqrt(v_hat) + ADAM_EPS)
+    step = (LEARN_RATE / (1.0 - BETA_ONE ** STEP_COUNT)) * moment_new
+    v_hat = sq_new * (1.0 / (1.0 - BETA_TWO ** STEP_COUNT))
+    weight_new = weight * (1.0 - LEARN_RATE * WEIGHT_DECAY) - step / (jnp.sqrt(v_hat) + ADAM_EPS)
     return weight_new, moment_new, sq_new
 
 
@@ -70,14 +71,17 @@
 
 def step_kernel(w1, w2, m1, m2, v1, v2, acc1, acc2, a_in, gy_in, x_in, maxn,
                 g1_o, g2_o, nrm_o, y_o,
-                recv1, recv2, own1, own2, b1, b2, gp, hid, dz, abuf, gbuf, gnext, xbuf, ybuf, sq1, sq2, nbuf, nres,
+                recv1, recv2, own1, own2, b1, b2, gp, hid, dz, abuf, gbuf, gnext, xbuf, ybuf, sq1, sq2, nbuf, nplane,
                 a_snd, a_rcv, in_snd, in_rcv, g_snd, g_rcv, x_snd, x_rcv, y_snd, y_rcv, rs_snd, rs_rcv, ag_snd, ag_rcv,
-                n_snd, n_rcv, nt_snd, nt_rcv, ld, st, loc):
+                n_snd, n_rcv, np_snd, np_rcv, nt_snd, nt_rcv, ld, st, loc):
     r = lax.axis_index("data")
     s = lax.axis_index("stage")
     own_r = owner_of(s)
     away = 1 - 2 * (own_r // 3)
     d = (r - own_r) * away
+    partner = s + 1 - 2 * (s % 2)
+    pair, plane = s // 2, r // 3
+    early = EARLY[0] + (EARLY[1] - EARLY[0]) * (s % 2)
     accs, recvs, owns, gouts = (acc1, acc2), (recv1, recv2), (own1, own2), (g1_o, g2_o)
     heights = (R1, R2)
 
@@ -102,6 +106,29 @@
     def gathered(dst, rcv):
         for q in range(REPLICAS):
             arrive(dst.at[pl.ds(q * TOK, TOK), :], rcv.at[q])
+
+    barrier = pltpu.get_barrier_semaphore()
+    for q in range(1, REPLICAS):
+        pl.semaphore_signal(barrier, inc=1, device_id=((r + q) % REPLICAS, s), device_id_type=MESH)
+
+    @pl.when(d == 0)
+    def _():
+        for t in range(1, STAGES):
+            peer = (s + t) % STAGES
+            pl.semaphore_signal(barrier, inc=1, device_id=(owner_of(peer), peer), device_id_type=MESH)
+
+    @pl.when(s != STAGES - 1)
+    def _():
+        pl.semaphore_signal(barrier, inc=1, device_id=(r, STAGES - 1), device_id_type=MESH)
+
+    at_end = (r == 0) | (r == REPLICAS - 1)
+
+    @pl.when(at_end)
+    def _():
+        pl.semaphore_signal(barrier, inc=1, device_id=(r, partner), device_id_type=MESH)
+
+    signals = REPLICAS - 1 + jnp.where(at_end, 1, 0) + jnp.where(d == 0, STAGES - 1, 0) + jnp.where(s == STAGES - 1, STAGES - 1, 0)
+    pl.semaphore_wait(barrier, signals)
 
     @pl.when(s == STAGES - 1)
     def _():
@@ -119,7 +146,7 @@
         return remote(src, part, rs_snd.at[sem], rs_rcv.at[sem], r - away, s)
 
     def rs_src(mat, k):
-        return accs[mat].at[0, 0, ds(k, heights[mat]), :]
+        return owns[mat].at[ds(k, heights[mat]), :]
 
     def ag_copy(mat, k, from_vmem):
         rows = ds(k, heights[mat])
@@ -127,6 +154,12 @@
         sem = mat * CHUNKS + k
         return remote(src.at[rows, :], gouts[mat].at[rows, :], ag_snd.at[sem], ag_rcv.at[sem], r + away, s)
 
+    def ag_range(lo, hi):
+        for mat in (0, 1):
+            @pl.loop(jnp.clip(lo - mat * CHUNKS, 0, CHUNKS), jnp.clip(hi - mat * CHUNKS, 0, CHUNKS))
+            def _(k):
+                ag_copy(mat, k, True).start()
+
     def each(mats, fn, lo=0, hi=CHUNKS):
         for mat in mats:
             @pl.loop(lo, hi)
@@ -135,7 +168,17 @@
 
     @pl.when(d == 3)
     def _():
-        each((0, 1), lambda mat, k: rs_copy(mat, k, rs_src(mat, k)).start())
+        parts = 4
+        loads = [pltpu.make_async_copy(acc1.at[0, 0, pl.ds(q * D // parts, D // parts), :], own1.at[pl.ds(q * D // parts, D // parts), :], ld.at[0, q])
+                 for q in range(parts)]
+        loads.append(pltpu.make_async_copy(acc2.at[0, 0], own2, ld.at[1, 0]))
+        for copy in loads:
+            copy.start()
+        for q in range(parts):
+            loads[q].wait()
+            each((0,), lambda mat, k: rs_copy(mat, k, rs_src(mat, k)).start(), q * CHUNKS // parts, (q + 1) * CHUNKS // parts)
+        loads[parts].wait()
+        each((1,), lambda mat, k: rs_copy(mat, k, rs_src(mat, k)).start())
 
     @pl.when((d == 1) | (d == 2))
     def _():
@@ -152,6 +195,14 @@
                 recvs[mat][rows, :] = recvs[mat][rows, :] + owns[mat][rows, :]
                 rs_copy(mat, k, recvs[mat].at[rows, :]).start()
 
+    @pl.when(d == 3)
+    def _():
+        arrive(nplane.at[plane], np_rcv.at[0])
+        remote(nplane.at[plane], nplane.at[plane], np_snd.at[0], np_rcv.at[1], own_r, s).start()
+        arrive(nplane.at[1 - plane], np_rcv.at[2])
+        for q in (1, 2):
+            remote(nplane, nplane, nt_snd.at[q], nt_rcv, own_r + q * away, s).start()
+
     @pl.when(d != 0)
     def _():
         for mat in (0, 1):
@@ -171,7 +222,16 @@
                         for t in range(1, STAGES):
                             remote(y_o, y_o, y_snd.at[t], y_rcv, r, (s + t) % STAGES).start()
 
-        arrive(nres, nt_rcv)
+        @pl.when(d != 3)
+        def _():
+            arrive(nplane, nt_rcv)
+
+        @pl.when(d == 3)
+        def _():
+            remote(nplane.at[plane], nplane.at[plane], np_snd.at[0], np_rcv.at[1], own_r, s).wait_send()
+            for q in (1, 2):
+                remote(nplane, nplane, nt_snd.at[q], nt_rcv, own_r + q * away, s).wait_send()
+
         remote(a_in, abuf.at[ds(r, TOK), :], a_snd, a_rcv.at[r], own_r, s).wait_send()
 
         @pl.when((s == 0) | (s == STAGES - 1))
@@ -267,40 +327,32 @@
                     part = part + avg[8 * i:8 * i + 8, :] * avg[8 * i:8 * i + 8, :]
                 sq[...] = sq[...] + part
                 if mat == 1:
-                    @pl.when(k >= CHUNKS - EARLY)
+                    @pl.when(k >= CHUNKS - early)
                     def _():
-                        ag_copy(0, k - (CHUNKS - EARLY), True).start()
+                        ag_copy(0, k - (CHUNKS - early), True).start()
+
+        chained = (s % 2 == 0) | (s == STAGES - 1)
+        first = jnp.where(chained, 34 + 6 * s - 6 * (s // 7), 2 * CHUNKS)
+        second = jnp.where(chained, first + 3, 2 * CHUNKS)
+        ag_range(early, first)
 
         partial = jnp.sum(sq1[...], keepdims=True) + jnp.sum(sq2[...], keepdims=True)
-        nbuf[s] = jnp.broadcast_to(partial, (8, 128))
+        nbuf[pair] = jnp.broadcast_to(partial, (8, 128))
         norm_copies = []
-        for t in range(1, STAGES):
-            peer = (s + t) % STAGES
-            norm_copies.append(remote(nbuf.at[s], nbuf.at[s], n_snd.at[t], n_rcv.at[s], owner_of(peer), peer))
+        for q in range(1, REPLICAS):
+            other = (pair + q) % REPLICAS
+            norm_copies.append(remote(nbuf.at[pair], nbuf.at[pair], n_snd.at[q], n_rcv.at[pair], r, 2 * other + (other + plane) % 2))
             norm_copies[-1].start()
-        for t in range(1, STAGES):
-            peer = (s + t) % STAGES
-            arrive(nbuf.at[peer], n_rcv.at[peer])
-        total = nbuf[0]
-        for t in range(1, STAGES):
-            total = total + nbuf[t]
-        nres[...] = total
-        total_copies = [remote(nres, nres, nt_snd.at[q], nt_rcv, own_r + q * away, s) for q in range(1, REPLICAS)]
-        for copy in total_copies:
-            copy.start()
-
-        chained = (s % 2 == 0) | (s == STAGES - 1)
-        first = jnp.where(chained, 8 + 2 * s, CHUNKS)
-
-        @pl.loop(EARLY, first)
-        def _(k):
-            ag_copy(0, k, True).start()
-
-        @pl.when(jnp.logical_not(chained))
-        def _():
-            @pl.loop(0, CHUNKS)
-            def _(k):
-                ag_copy(1, k, True).start()
+        for q in range(1, REPLICAS):
+            other = (pair + q) % REPLICAS
+            arrive(nbuf.at[other], n_rcv.at[other])
+        nplane[plane] = (nbuf[0] + nbuf[1]) + (nbuf[2] + nbuf[3])
+        norm_copies.append(remote(nplane.at[plane], nplane.at[plane], np_snd.at[0], np_rcv.at[0], r, partner))
+        norm_copies[-1].start()
+        arrive(nplane.at[1 - plane], np_rcv.at[1])
+        norm_copies.append(remote(nplane.at[1 - plane], nplane.at[1 - plane], np_snd.at[1], np_rcv.at[2], r, partner))
+        norm_copies[-1].start()
+        total = nplane[0] + nplane[1]
 
         local_copies = [pltpu.make_async_copy(recvs[mat], gouts[mat], loc.at[mat]) for mat in (0, 1)]
         for copy in local_copies:
@@ -340,6 +392,8 @@
         def _():
             arrive(xbuf, x_rcv)
 
+        ag_range(first, second)
+
         @pl.loop(0, FF // TILE)
         def _(j):
             cols = ds(j, TILE)
@@ -367,15 +421,7 @@
             for t in range(1, STAGES):
                 remote(y_o, y_o, y_snd.at[t], y_rcv, r, (s + t) % STAGES).start()
 
-        @pl.when(chained)
-        def _():
-            @pl.loop(first, CHUNKS)
-            def _(k):
-                ag_copy(0, k, True).start()
-
-            @pl.loop(0, CHUNKS)
-            def _(k):
-                ag_copy(1, k, True).start()
+        ag_range(second, 2 * CHUNKS)
 
         @pl.when(s == STAGES - 1)
         def _():
@@ -390,13 +436,13 @@
         def _():
             send_x.wait_send()
 
-        for copy in norm_copies + total_copies:
+        for copy in norm_copies:
             copy.wait_send()
         for copy in local_copies:
             copy.wait()
         each((0, 1), lambda mat, k: ag_copy(mat, k, True).wait_send())
 
-    nrm_o[...] = nres[...]
+    nrm_o[...] = nplane[0] + nplane[1]
 
     @pl.when(s != STAGES - 1)
     def _():
@@ -443,24 +489,25 @@
                 pltpu.VMEM((ROWS, D), BF16), pltpu.VMEM((ROWS, D), BF16), pltpu.VMEM((ROWS, D), BF16),
                 pltpu.VMEM((ROWS, D), BF16), pltpu.VMEM((ROWS, D), BF16),
                 pltpu.VMEM((8, FF), F32), pltpu.VMEM((8, D), F32),
-                pltpu.VMEM((STAGES, 8, 128), F32), pltpu.VMEM((8, 128), F32),
+                pltpu.VMEM((REPLICAS, 8, 128), F32), pltpu.VMEM((2, 8, 128), F32),
                 dma, dma((REPLICAS,)), dma, dma((REPLICAS,)), dma, dma, dma, dma, dma((STAGES + REPLICAS,)), dma,
                 dma((2 * CHUNKS,)), dma((2 * CHUNKS,)), dma((2 * CHUNKS,)), dma((2 * CHUNKS,)),
-                dma((STAGES,)), dma((STAGES,)), dma((REPLICAS,)), dma,
-                dma((2, 2)), dma((2, 3 * SLOTS)), dma((3,)),
+                dma((REPLICAS,)), dma((REPLICAS,)), dma((2,)), dma((3,)), dma((REPLICAS,)), dma,
+                dma((2, 4)), dma((2, 3 * SLOTS)), dma((3,)),
             ],
-            compiler_params=pltpu.CompilerParams(has_side_effects=True, vmem_limit_bytes=67043328),
+            compiler_params=pltpu.CompilerParams(has_side_effects=True, collective_id=0, vmem_limit_bytes=67043328),
             name="reduce_backward_broadcast_forward",
         )(w_in, w_out, mom_in, mom_out, sq_in, sq_out, acc_in, acc_out, stage_acts[0], grad_y, x_next[0], maxn)
 
         one = pl.BlockSpec((8, 128), lambda k: (0, 0))
-        wide = pl.BlockSpec((1, R1, FF), lambda k: (0, k, 0))
-        tall = pl.BlockSpec((1, R2, D), lambda k: (0, k, 0))
+        short, high = D // UPDATES, FF // UPDATES
+        wide = pl.BlockSpec((1, short, FF), lambda k: (0, k, 0))
+        tall = pl.BlockSpec((1, high, D), lambda k: (0, k, 0))
         new = pl.pallas_call(
             update_kernel,
-            grid=(CHUNKS,),
+            grid=(UPDATES,),
             out_shape=[jax.ShapeDtypeStruct((1, D, FF), F32)] * 3 + [jax.ShapeDtypeStruct((1, FF, D), F32)] * 3,
-            in_specs=[one, one] + [wide] * 3 + [pl.BlockSpec((R1, FF), lambda k: (k, 0))] + [tall] * 3 + [pl.BlockSpec((R2, D), lambda k: (k, 0))],
+            in_specs=[one, one] + [wide] * 3 + [pl.BlockSpec((short, FF), lambda k: (k, 0))] + [tall] * 3 + [pl.BlockSpec((high, D), lambda k: (k, 0))],
             out_specs=[wide] * 3 + [tall] * 3,
             name="adamw_update",
         )(nrm, maxn, w_in, mom_in, sq_in, g1, w_out, mom_out, sq_out, g2)

time: 553 us -> 503 us (0.910)
  Pallas kernels: 551 us -> 499 us
    pallas_call x1, Pallas kernels: 500 us -> 454 us  [local_step(): pl.pallas_call(step_kernel, out_shape=(jax.ShapeDtypeStruct((D, FF), F32)...]
where the time goes in v2:
time: 503 us; the launch traced here: 502 us
  Pallas kernels  499 us (99%)
    pallas_call x1, Pallas kernels, local_step(): pl.pallas_call(step_kernel, out_shape=(jax.ShapeDtypeStruct((D, FF), F32)...  454 us
    pallas_call x1, Pallas kernels, local_step(): pl.pallas_call(update_kernel, grid=(UPDATES,), out_shape=[jax.ShapeDtypeS...  45.6 us

profile of v2, /device:TPU:31, one launch (start us, length us, event | category | flops | bytes accessed | tf_op | source)
XLA Modules:
  0.0 501.9 jit_solution(9727014775296159249)
XLA Ops:
  1.3 0.6 broadcast_in_dim.6.maxn
  1.9 453.8 %reduce_backward_broadcast_forward.1 = (f32[768,3072]{1,0:T(8,128)}, f32[3072,768]{1,0:T(8,128)}, f32[8,128]{1,0:T(8,128)}, bf16[64,768]{1,0:T(8,128)(2,1)}) custom-call(f32[1,768,3072]{2,1,0:T(8,128)} %refs_0_.1, f32[1,3072,768]{2,1,0:T(8,128)} %refs_4_.1, f32[1,768,3072]{2,1,0:T(8,128)} %refs_1_.1, f32[1,3072,768]{2,1,0:T(8,128)} %refs_5_.1, ...), custom_call_target="tpu_custom_call" | custom-call | tf_op jit(solution)/shard_map/reduce_backward_broadcast_forward/pallas_call | solution.py:476
  455.7 0.0 copy-start
  455.7 45.6 %adamw_update.1 = (f32[1,768,3072]{2,1,0:T(8,128)}, f32[1,768,3072]{2,1,0:T(8,128)}, f32[1,768,3072]{2,1,0:T(8,128)}, f32[1,3072,768]{2,1,0:T(8,128)}, f32[1,3072,768]{2,1,0:T(8,128)}, /*index=5*/f32[1,3072,768]{2,1,0:T(8,128)}) custom-call(f32[8,128]{1,0:T(8,128)} %get-tuple-element.17.nrm, f32[8,128]{1,0:T(8,128)} %broadcast_in_dim.6.maxn, ...), custom_call_target="tpu_custom_call" | custom-call | tf_op jit(solution)/shard_map/adamw_update/pallas_call | solution.py:506
  501.3 0.0 copy-done
  501.3 0.6 copy.21
Async XLA Ops:
  455.7 45.6 %copy-start = (bf16[64,768]{1,0:T(8,128)(2,1)S(1)}, bf16[64,768]{1,0:T(8,128)(2,1)}, u32[]{:S(2)}) copy-start(bf16[64,768]{1,0:T(8,128)(2,1)} %get-tuple-element.26) | copy-start | bytes 294916

commit v3 on v2

--- a/solution.py
+++ b/solution.py
@@ -21,10 +21,12 @@
 ROWS = REPLICAS * TOK
 CHUNKS = 48
 R1, R2 = D // CHUNKS, FF // CHUNKS
-UPDATES = 16
+LAG = 16
 TILE = 256
-SLOTS = 16
-EARLY = (16, 2)
+SLOTS = 8
+EARLY = (9, 4)
+VMEM_LIMIT = 19800000
+FLUSH = 4
 LEARN_RATE = LR_GAIN * D ** -0.5
 GELU_K = math.sqrt(2.0 / math.pi)
 NT = (((1,), (1,)), ((), ()))
@@ -52,13 +54,14 @@
     return jnp.minimum(1.0, max_norm / (jnp.sqrt(sq_norm) + CLIP_EPS))
 
 
-def adamw(weight, moment, sq_moment, gradient):
-    moment_new = BETA_ONE * moment + (1.0 - BETA_ONE) * gradient
-    sq_new = BETA_TWO * sq_moment + (1.0 - BETA_TWO) * gradient * gradient
+def moments(moment, sq_moment, gradient):
+    return BETA_ONE * moment + (1.0 - BETA_ONE) * gradient, BETA_TWO * sq_moment + (1.0 - BETA_TWO) * gradient * gradient
+
+
+def new_weight(weight, moment_new, sq_new):
     step = (LEARN_RATE / (1.0 - BETA_ONE ** STEP_COUNT)) * moment_new
     v_hat = sq_new * (1.0 / (1.0 - BETA_TWO ** STEP_COUNT))
-    weight_new = weight * (1.0 - LEARN_RATE * WEIGHT_DECAY) - step / (jnp.sqrt(v_hat) + ADAM_EPS)
-    return weight_new, moment_new, sq_new
+    return weight * (1.0 - LEARN_RATE * WEIGHT_DECAY) - step / (jnp.sqrt(v_hat) + ADAM_EPS)
 
 
 def owner_of(stage):
@@ -70,10 +73,10 @@
 
 
 def step_kernel(w1, w2, m1, m2, v1, v2, acc1, acc2, a_in, gy_in, x_in, maxn,
-                g1_o, g2_o, nrm_o, y_o,
-                recv1, recv2, own1, own2, b1, b2, gp, hid, dz, abuf, gbuf, gnext, xbuf, ybuf, sq1, sq2, nbuf, nplane,
+                recv1, recv2, own1, own2, sq_o, v2_o, g1_o, g2_o, y_o,
+                b1, b2, hid, ring1, ring2, ringv, abuf, gbuf, gnext, xbuf, ybuf, sq1, sq2, nbuf, nplane,
                 a_snd, a_rcv, in_snd, in_rcv, g_snd, g_rcv, x_snd, x_rcv, y_snd, y_rcv, rs_snd, rs_rcv, ag_snd, ag_rcv,
-                n_snd, n_rcv, np_snd, np_rcv, nt_snd, nt_rcv, ld, st, loc):
+                n_snd, n_rcv, np_snd, np_rcv, nt_snd, nt_rcv, ld, st, vo, loc):
     r = lax.axis_index("data")
     s = lax.axis_index("stage")
     own_r = owner_of(s)
@@ -83,7 +86,9 @@
     pair, plane = s // 2, r // 3
     early = EARLY[0] + (EARLY[1] - EARLY[0]) * (s % 2)
     accs, recvs, owns, gouts = (acc1, acc2), (recv1, recv2), (own1, own2), (g1_o, g2_o)
+    rings, weights_hbm, moments_hbm = (ring1, ring2), (w1, w2), (m1, m2)
     heights = (R1, R2)
+    gp, dz = sq_o.at[pl.ds(0, ROWS), :], sq_o.at[pl.ds(ROWS, ROWS), :]
 
     def remote(src, dst, snd, rcv, to_r, to_s):
         return pltpu.make_async_remote_copy(src_ref=src, dst_ref=dst, send_sem=snd, recv_sem=rcv,
@@ -195,36 +200,128 @@
                 recvs[mat][rows, :] = recvs[mat][rows, :] + owns[mat][rows, :]
                 rs_copy(mat, k, recvs[mat].at[rows, :]).start()
 
-    @pl.when(d == 3)
-    def _():
-        arrive(nplane.at[plane], np_rcv.at[0])
-        remote(nplane.at[plane], nplane.at[plane], np_snd.at[0], np_rcv.at[1], own_r, s).start()
-        arrive(nplane.at[1 - plane], np_rcv.at[2])
-        for q in (1, 2):
-            remote(nplane, nplane, nt_snd.at[q], nt_rcv, own_r + q * away, s).start()
+    def load(mat, k, src, ring, sem):
+        slot = k % SLOTS
+        return pltpu.make_async_copy(src, ring.at[slot], st.at[sem * SLOTS + slot])
+
+    def load_rows(mat, k, hbm):
+        return load(mat, k, hbm.at[ds(k, heights[mat]), :], rings[mat], mat)
+
+    def load_v2(k, hbm):
+        return load(1, k, hbm.at[ds(k, R2), :], ringv, 2)
+
+    def store_v2(k):
+        return pltpu.make_async_copy(ringv.at[k % SLOTS], v2_o.at[ds(k, R2), :], vo.at[k % SLOTS])
+
+    def whole(mat, src, dst, sem):
+        return pltpu.make_async_copy(src.at[0], dst, ld.at[mat, sem])
 
     @pl.when(d != 0)
     def _():
-        for mat in (0, 1):
-            @pl.loop(0, CHUNKS)
-            def _(k):
-                rows = ds(k, heights[mat])
-                arrive(gouts[mat].at[rows, :], ag_rcv.at[mat * CHUNKS + k])
-
-                @pl.when(d != 3)
-                def _():
-                    ag_copy(mat, k, False).start()
-
-                if mat == 1:
-                    @pl.when((s == STAGES - 1) & (k == CHUNKS - 8))
-                    def _():
-                        arrive(y_o, y_rcv)
-                        for t in range(1, STAGES):
-                            remote(y_o, y_o, y_snd.at[t], y_rcv, r, (s + t) % STAGES).start()
+        fills = ([whole(0, w1, recv1, 0), whole(0, m1, own1, 1), whole(0, v1, sq_o, 2)], [whole(1, w2, recv2, 0), whole(1, m2, own2, 1)])
+
+        def prefetch():
+            each((0, 1), lambda mat, k: rs_copy(mat, k, rs_src(mat, k)).wait_send())
+            for copy in fills[0] + fills[1]:
+                copy.start()
+
+        def pass_on(mat, k):
+            rows = ds(k, heights[mat])
+            arrive(gouts[mat].at[rows, :], ag_rcv.at[mat * CHUNKS + k])
+
+            @pl.when(d != 3)
+            def _():
+                ag_copy(mat, k, False).start()
+
+        @pl.when(d == 3)
+        def _():
+            prefetch()
+            arrive(nplane.at[plane], np_rcv.at[0])
+            remote(nplane.at[plane], nplane.at[plane], np_snd.at[0], np_rcv.at[1], own_r, s).start()
+            arrive(nplane.at[1 - plane], np_rcv.at[2])
+            for q in (1, 2):
+                remote(nplane, nplane, nt_snd.at[q], nt_rcv, own_r + q * away, s).start()
+
+        each((0,), pass_on, 0, LAG // 2)
 
         @pl.when(d != 3)
         def _():
+            prefetch()
+
+        each((0,), pass_on, LAG // 2, LAG)
+
+        @pl.when(d != 3)
+        def _():
             arrive(nplane, nt_rcv)
+
+        clip = clip_of(nplane[0] + nplane[1], maxn[...])[0:1, 0:1]
+        for copy in fills[0]:
+            copy.wait()
+
+        def update_first(k):
+            load_rows(0, k, g1_o).wait()
+            rows = ds(k, R1)
+            moment, sq_moment = moments(own1[rows, :], sq_o[rows, :], clip * ring1[k % SLOTS])
+            recv1[rows, :] = new_weight(recv1[rows, :], moment, sq_moment)
+            own1[rows, :] = moment
+            sq_o[rows, :] = sq_moment
+
+        def update_second(k):
+            load_rows(1, k, g2_o).wait()
+            load_v2(k, v2.at[0]).wait()
+            rows = ds(k, R2)
+            moment, sq_moment = moments(own2[rows, :], ringv[k % SLOTS], clip * ring2[k % SLOTS])
+            recv2[rows, :] = new_weight(recv2[rows, :], moment, sq_moment)
+            own2[rows, :] = moment
+            ringv[k % SLOTS] = sq_moment
+            store_v2(k).start()
+
+        @pl.loop(LAG, 2 * LAG)
+        def _(k):
+            pass_on(0, k)
+            for i in (0, 1):
+                load_rows(0, 2 * (k - LAG) + i, g1_o).start()
+
+            @pl.when(k > LAG)
+            def _():
+                for i in (0, 1):
+                    update_first(2 * (k - LAG - 1) + i)
+
+        update_first(2 * LAG - 2)
+
+        @pl.loop(2 * LAG, CHUNKS)
+        def _(k):
+            pass_on(0, k)
+            load_rows(0, k, g1_o).start()
+            update_first(k - 1)
+
+        update_first(CHUNKS - 1)
+        for copy in fills[1]:
+            copy.wait()
+
+        @pl.loop(0, CHUNKS)
+        def _(k):
+            pass_on(1, k)
+
+            @pl.when(k >= SLOTS)
+            def _():
+                store_v2(k - SLOTS).wait()
+
+            load_rows(1, k, g2_o).start()
+            load_v2(k, v2.at[0]).start()
+
+            @pl.when(k > 0)
+            def _():
+                update_second(k - 1)
+
+            @pl.when((s == STAGES - 1) & (k == CHUNKS - 8))
+            def _():
+                arrive(y_o, y_rcv)
+                for t in range(1, STAGES):
+                    remote(y_o, y_o, y_snd.at[t], y_rcv, r, (s + t) % STAGES).start()
+
+        update_second(CHUNKS - 1)
+        each((1,), lambda mat, k: store_v2(k).wait(), CHUNKS - SLOTS, CHUNKS)
 
         @pl.when(d == 3)
         def _():
@@ -237,8 +334,6 @@
         @pl.when((s == 0) | (s == STAGES - 1))
         def _():
             remote(x_in, xbuf.at[ds(r, TOK), :], in_snd, in_rcv.at[r], own_r, s).wait_send()
-
-        each((0, 1), lambda mat, k: rs_copy(mat, k, rs_src(mat, k)).wait_send())
 
         @pl.when(d != 3)
         def _():
@@ -287,7 +382,7 @@
         @pl.loop(0, FF // TILE)
         def _(j):
             cols = ds(j, TILE)
-            dz[:, cols] = (gp[:, cols] * mm(gbuf[...], b2[cols, :], NT)).astype(BF16)
+            dz[:, cols] = (gp[:, cols] * mm(gbuf[...], b2[cols, :], NT)).astype(BF16).astype(F32)
 
         send_g = remote(gnext, gbuf, g_snd, g_rcv, owner_of(s + STAGES - 1), (s + STAGES - 1) % STAGES)
 
@@ -295,7 +390,7 @@
         def _():
             @pl.loop(0, D // TILE)
             def _(j):
-                gnext[:, ds(j, TILE)] = mm(dz[...], b1[ds(j, TILE), :], NT).astype(BF16)
+                gnext[:, ds(j, TILE)] = mm(dz[...].astype(BF16), b1[ds(j, TILE), :], NT).astype(BF16)
 
             send_g.start()
 
@@ -304,7 +399,7 @@
         @pl.loop(0, FF // TILE)
         def _(j):
             cols = ds(j, TILE)
-            own1[:, cols] = own1[:, cols] + mm(abuf[...], dz[:, cols], TN)
+            own1[:, cols] = own1[:, cols] + mm(abuf[...], dz[:, cols].astype(BF16), TN)
 
         own_copies[1].wait()
 
@@ -332,9 +427,17 @@
                         ag_copy(0, k - (CHUNKS - early), True).start()
 
         chained = (s % 2 == 0) | (s == STAGES - 1)
-        first = jnp.where(chained, 34 + 6 * s - 6 * (s // 7), 2 * CHUNKS)
+        first = jnp.where(chained, 26 + 6 * s + s // 4 - 2 * (s // 7), 2 * CHUNKS)
         second = jnp.where(chained, first + 3, 2 * CHUNKS)
         ag_range(early, first)
+
+        fills = [whole(0, m1, own1, 2), whole(0, v1, sq_o, 3), whole(1, m2, own2, 2)]
+        for copy in fills:
+            copy.start()
+        for k in range(SLOTS):
+            load_rows(0, k, w1.at[0]).start()
+            load_rows(1, k, w2.at[0]).start()
+            load_v2(k, v2.at[0]).start()
 
         partial = jnp.sum(sq1[...], keepdims=True) + jnp.sum(sq2[...], keepdims=True)
         nbuf[pair] = jnp.broadcast_to(partial, (8, 128))
@@ -354,35 +457,44 @@
         norm_copies[-1].start()
         total = nplane[0] + nplane[1]
 
-        local_copies = [pltpu.make_async_copy(recvs[mat], gouts[mat], loc.at[mat]) for mat in (0, 1)]
-        for copy in local_copies:
-            copy.start()
-
         clip = clip_of(total, maxn[...])[0:1, 0:1]
-        for mat, (weights, hbm) in enumerate(((b1, (w1, m1, v1)), (b2, (w2, m2, v2)))):
-            height = heights[mat]
-
-            def fetch(k, i):
-                slot = (k % SLOTS) * 3 + i
-                return pltpu.make_async_copy(hbm[i].at[0, ds(k, height), :], owns[mat].at[ds(slot, height), :], st.at[mat, slot])
-
-            for k in range(SLOTS):
-                for i in range(3):
-                    fetch(k, i).start()
-
-            @pl.loop(0, CHUNKS)
-            def _(k):
-                for i in range(3):
-                    fetch(k, i).wait()
-                rows = ds(k, height)
-                parts = [owns[mat][ds((k % SLOTS) * 3 + i, height), :] for i in range(3)]
-                new_weight, _, _ = adamw(*parts, clip * recvs[mat][rows, :])
-                weights[rows, :] = new_weight.astype(BF16)
-
-                @pl.when(k + SLOTS < CHUNKS)
-                def _():
-                    for i in range(3):
-                        fetch(k + SLOTS, i).start()
+        for copy in fills:
+            copy.wait()
+
+        @pl.loop(0, CHUNKS)
+        def _(k):
+            load_rows(0, k, w1.at[0]).wait()
+            rows = ds(k, R1)
+            moment, sq_moment = moments(own1[rows, :], sq_o[rows, :], clip * recv1[rows, :])
+            b1[rows, :] = new_weight(ring1[k % SLOTS], moment, sq_moment).astype(BF16)
+            own1[rows, :] = moment
+            sq_o[rows, :] = sq_moment
+
+            @pl.when(k + SLOTS < CHUNKS)
+            def _():
+                load_rows(0, k + SLOTS, w1.at[0]).start()
+
+        @pl.loop(0, CHUNKS)
+        def _(k):
+            load_rows(1, k, w2.at[0]).wait()
+            load_v2(k, v2.at[0]).wait()
+            rows = ds(k, R2)
+            moment, sq_moment = moments(own2[rows, :], ringv[k % SLOTS], clip * recv2[rows, :])
+            b2[rows, :] = new_weight(ring2[k % SLOTS], moment, sq_moment).astype(BF16)
+            own2[rows, :] = moment
+            ringv[k % SLOTS] = sq_moment
+            store_v2(k).start()
+
+            @pl.when(k + SLOTS < CHUNKS)
+            def _():
+                load_rows(1, k + SLOTS, w2.at[0]).start()
+
+            @pl.when((k >= SLOTS // 2) & (k + SLOTS // 2 < CHUNKS))
+            def _():
+                store_v2(k - SLOTS // 2).wait()
+                load_v2(k + SLOTS // 2, v2.at[0]).start()
+
+        each((1,), lambda mat, k: store_v2(k).wait(), CHUNKS - SLOTS, CHUNKS)
 
         @pl.when(s == 0)
         def _():
@@ -438,11 +550,35 @@
 
         for copy in norm_copies:
             copy.wait_send()
-        for copy in local_copies:
-            copy.wait()
-        each((0, 1), lambda mat, k: ag_copy(mat, k, True).wait_send())
-
-    nrm_o[...] = nplane[0] + nplane[1]
+
+        for k in range(SLOTS):
+            load_rows(0, k, w1.at[0]).start()
+            load_rows(1, k, w2.at[0]).start()
+            load_v2(k, v2_o).start()
+
+        @pl.loop(0, CHUNKS)
+        def _(k):
+            ag_copy(0, k, True).wait_send()
+            load_rows(0, k, w1.at[0]).wait()
+            rows = ds(k, R1)
+            recv1[rows, :] = new_weight(ring1[k % SLOTS], own1[rows, :], sq_o[rows, :])
+
+            @pl.when(k + SLOTS < CHUNKS)
+            def _():
+                load_rows(0, k + SLOTS, w1.at[0]).start()
+
+        @pl.loop(0, CHUNKS)
+        def _(k):
+            ag_copy(1, k, True).wait_send()
+            load_rows(1, k, w2.at[0]).wait()
+            load_v2(k, v2_o).wait()
+            rows = ds(k, R2)
+            recv2[rows, :] = new_weight(ring2[k % SLOTS], own2[rows, :], ringv[k % SLOTS])
+
+            @pl.when(k + SLOTS < CHUNKS)
+            def _():
+                load_rows(1, k + SLOTS, w2.at[0]).start()
+                load_v2(k + SLOTS, v2_o).start()
 
     @pl.when(s != STAGES - 1)
     def _():
@@ -454,13 +590,25 @@
             remote(y_o, y_o, y_snd.at[t], y_rcv, r, (s + t) % STAGES).wait_send()
 
 
-def update_kernel(nrm, maxn, *refs):
-    clip = clip_of(nrm[...], maxn[...])[0:1, 0:1]
-    for mat in (0, 1):
-        weight, moment, sq_moment, grad = (ref[...] for ref in refs[4 * mat:4 * mat + 4])
-        new = adamw(weight[0], moment[0], sq_moment[0], clip * grad)
-        for ref, value in zip(refs[8 + 3 * mat:11 + 3 * mat], new):
-            ref[0] = value
+def flush_kernel(*refs):
+    source, target, (buf, rsem, wsem) = refs[5], refs[11], refs[12:]
+    keep = pltpu.make_async_copy(refs[4], refs[10], wsem.at[FLUSH])
+    keep.start()
+    height = FF // FLUSH
+
+    def copies(k):
+        rows = pl.ds(k * height, height)
+        return (pltpu.make_async_copy(source.at[rows, :], buf.at[rows, :], rsem.at[k]),
+                pltpu.make_async_copy(buf.at[rows, :], target.at[rows, :], wsem.at[k]))
+
+    for k in range(FLUSH):
+        copies(k)[0].start()
+    for k in range(FLUSH):
+        copies(k)[0].wait()
+        copies(k)[1].start()
+    for k in range(FLUSH):
+        copies(k)[1].wait()
+    keep.wait()
 
 
 def solution(mesh):
@@ -473,19 +621,19 @@
         hbm = pl.BlockSpec(memory_space=pl.ANY)
         vmem = pl.BlockSpec(memory_space=pltpu.VMEM)
         dma = pltpu.SemaphoreType.DMA
-        g1, g2, nrm, y = pl.pallas_call(
+        wide, tall = pltpu.VMEM((D, FF), F32), pltpu.VMEM((FF, D), F32)
+        *kept, sq_out_new, _, _, y_next = pl.pallas_call(
             step_kernel,
             out_shape=(
-                jax.ShapeDtypeStruct((D, FF), F32), jax.ShapeDtypeStruct((FF, D), F32),
-                jax.ShapeDtypeStruct((8, 128), F32), jax.ShapeDtypeStruct((TOK, D), BF16),
+                wide, tall, wide, tall, wide,
+                jax.ShapeDtypeStruct((FF, D), F32), jax.ShapeDtypeStruct((D, FF), F32), jax.ShapeDtypeStruct((FF, D), F32),
+                jax.ShapeDtypeStruct((TOK, D), BF16),
             ),
             in_specs=[hbm] * 11 + [vmem],
-            out_specs=(hbm, hbm, vmem, hbm),
+            out_specs=(vmem,) * 5 + (hbm,) * 4,
             scratch_shapes=[
-                pltpu.VMEM((D, FF), F32), pltpu.VMEM((FF, D), F32),
-                pltpu.VMEM((D, FF), F32), pltpu.VMEM((FF, D), F32),
-                pltpu.VMEM((D, FF), BF16), pltpu.VMEM((FF, D), BF16),
-                pltpu.VMEM((ROWS, FF), F32), pltpu.VMEM((ROWS, FF), BF16), pltpu.VMEM((ROWS, FF), BF16),
+                pltpu.VMEM((D, FF), BF16), pltpu.VMEM((FF, D), BF16), pltpu.VMEM((ROWS, FF), BF16),
+                pltpu.VMEM((SLOTS, R1, FF), F32), pltpu.VMEM((SLOTS, R2, D), F32), pltpu.VMEM((SLOTS, R2, D), F32),
                 pltpu.VMEM((ROWS, D), BF16), pltpu.VMEM((ROWS, D), BF16), pltpu.VMEM((ROWS, D), BF16),
                 pltpu.VMEM((ROWS, D), BF16), pltpu.VMEM((ROWS, D), BF16),
                 pltpu.VMEM((8, FF), F32), pltpu.VMEM((8, D), F32),
@@ -493,25 +641,23 @@
                 dma, dma((REPLICAS,)), dma, dma((REPLICAS,)), dma, dma, dma, dma, dma((STAGES + REPLICAS,)), dma,
                 dma((2 * CHUNKS,)), dma((2 * CHUNKS,)), dma((2 * CHUNKS,)), dma((2 * CHUNKS,)),
                 dma((REPLICAS,)), dma((REPLICAS,)), dma((2,)), dma((3,)), dma((REPLICAS,)), dma,
-                dma((2, 4)), dma((2, 3 * SLOTS)), dma((3,)),
+                dma((2, 4)), dma((3 * SLOTS,)), dma((SLOTS,)), dma((3,)),
             ],
-            compiler_params=pltpu.CompilerParams(has_side_effects=True, collective_id=0, vmem_limit_bytes=67043328),
-            name="reduce_backward_broadcast_forward",
+            compiler_params=pltpu.CompilerParams(has_side_effects=True, collective_id=0, vmem_limit_bytes=VMEM_LIMIT),
+            name="step",
         )(w_in, w_out, mom_in, mom_out, sq_in, sq_out, acc_in, acc_out, stage_acts[0], grad_y, x_next[0], maxn)
-
-        one = pl.BlockSpec((8, 128), lambda k: (0, 0))
-        short, high = D // UPDATES, FF // UPDATES
-        wide = pl.BlockSpec((1, short, FF), lambda k: (0, k, 0))
-        tall = pl.BlockSpec((1, high, D), lambda k: (0, k, 0))
+        wide, tall = jax.ShapeDtypeStruct((D, FF), F32), jax.ShapeDtypeStruct((FF, D), F32)
         new = pl.pallas_call(
-            update_kernel,
-            grid=(UPDATES,),
-            out_shape=[jax.ShapeDtypeStruct((1, D, FF), F32)] * 3 + [jax.ShapeDtypeStruct((1, FF, D), F32)] * 3,
-            in_specs=[one, one] + [wide] * 3 + [pl.BlockSpec((short, FF), lambda k: (k, 0))] + [tall] * 3 + [pl.BlockSpec((high, D), lambda k: (k, 0))],
-            out_specs=[wide] * 3 + [tall] * 3,
-            name="adamw_update",
-        )(nrm, maxn, w_in, mom_in, sq_in, g1, w_out, mom_out, sq_out, g2)
-        return new[0], new[3], new[1], new[4], new[2], new[5], y[None]
+            flush_kernel,
+            out_shape=(wide, tall, wide, tall, wide, tall),
+            in_specs=[hbm] * 4 + [vmem, hbm],
+            out_specs=(hbm,) * 6,
+            input_output_aliases={i: i for i in range(4)},
+            scratch_shapes=[pltpu.VMEM((FF, D), F32), dma((FLUSH,)), dma((FLUSH + 1,))],
+            compiler_params=pltpu.CompilerParams(vmem_limit_bytes=10000000),
+            name="flush",
+        )(*kept[:4], pltpu.with_memory_space_constraint(kept[4], pltpu.VMEM), sq_out_new)
+        return *(array[None] for array in new), y_next[None]
 
     in_specs = (weight_spec,) * 6 + (acc_spec, acc_spec, P("stage", "data", None), P("data", None), P(None, "data", None), P())
     out_specs = (weight_spec,) * 6 + (P(None, "data", None),)

time: 503 us -> 473 us (0.940)
  Pallas kernels: 499 us -> 450 us
  local copies, waits for them, and re-layouts: 1.24 us -> 16.2 us
    pallas_call x2, Pallas kernels: 499 us -> 450 us  [the longest x1 439 us: local_step(): pl.pallas_call(step_kernel, out_shape=(wide, tall, wide, tall, wide, jax....]
    unnamed x3 -> x7, local copies, waits for them, and re-layouts: 0.65 us -> 15.6 us
where the time goes in v3:
time: 473 us; the launch traced here: 467 us
  Pallas kernels  450 us (95%)
  local copies, waits for them, and re-layouts  16.2 us (3%)
    pallas_call x1, Pallas kernels, local_step(): pl.pallas_call(step_kernel, out_shape=(wide, tall, wide, tall, wide, jax....  439 us
    unnamed x7, local copies, waits for them, and re-layouts  15.6 us
    pallas_call x1, Pallas kernels, local_step(): pl.pallas_call(flush_kernel, out_shape=(wide, tall, wide, tall, wide, tal...  10.3 us

profile of v3, /device:TPU:31, one launch (start us, length us, event | category | flops | bytes accessed | tf_op | source)
XLA Modules:
  0.0 467.1 jit_solution(8851080250108077171)
XLA Ops:
  1.3 0.6 broadcast_in_dim.24.maxn
  1.9 439.3 %step.1 = (f32[768,3072]{1,0:T(8,128)S(1)}, f32[3072,768]{1,0:T(8,128)S(1)}, f32[768,3072]{1,0:T(8,128)S(1)}, f32[3072,768]{1,0:T(8,128)S(1)}, f32[768,3072]{1,0...) custom-call(f32[1,768,3072]{2,1,0:T(8,128)} %w1.1, ...), custom_call_target="tpu_custom_call" | custom-call | tf_op jit(solution)/shard_map/step/pallas_call | solution.py:625
  441.2 10.3 %flush.1 = (f32[768,3072]{1,0:T(8,128)S(1)}, f32[3072,768]{1,0:T(8,128)S(1)}, f32[768,3072]{1,0:T(8,128)S(1)}, f32[3072,768]{1,0:T(8,128)S(1)}, f32[768,3072]{1,0:T(8,128)}, /*index=5*/f32[3072,768]{1,0:T(8,128)}) custom-call(f32[768,3072]{1,0:T(8,128)S(1)} %get-tuple-element.20.refs_0_, ...), custom_call_target="tpu_custom_call", output_to_operand_aliasing={{0}: (0, {}), {1}: (1, {}), {2}: (2, {}), {3}: (3, {})} | custom-call | tf_op jit(solution)/shard_map/flush/pallas_call | solution.py:650
  451.5 3.7 copy.32
  455.2 3.7 copy.33
  459.0 3.7 copy.34
  462.7 0.0 copy-start
  462.7 3.7 copy.35
  466.5 0.0 copy-done
  466.5 0.6 copy.37
Async XLA Ops:
  462.7 3.7 copy-start

commit v4 on v3

--- a/solution.py
+++ b/solution.py
@@ -21,10 +21,11 @@
 ROWS = REPLICAS * TOK
 CHUNKS = 48
 R1, R2 = D // CHUNKS, FF // CHUNKS
+GROUP = 8
 LAG = 16
 TILE = 256
 SLOTS = 8
-EARLY = (9, 4)
+EARLY = (8, 2)
 VMEM_LIMIT = 19800000
 FLUSH = 4
 LEARN_RATE = LR_GAIN * D ** -0.5
@@ -73,9 +74,9 @@
 
 
 def step_kernel(w1, w2, m1, m2, v1, v2, acc1, acc2, a_in, gy_in, x_in, maxn,
-                recv1, recv2, own1, own2, sq_o, v2_o, g1_o, g2_o, y_o,
+                recv2, own2, first_o, v2_o, g1_o, g2_o, y_o,
                 b1, b2, hid, ring1, ring2, ringv, abuf, gbuf, gnext, xbuf, ybuf, sq1, sq2, nbuf, nplane,
-                a_snd, a_rcv, in_snd, in_rcv, g_snd, g_rcv, x_snd, x_rcv, y_snd, y_rcv, rs_snd, rs_rcv, ag_snd, ag_rcv,
+                a_snd, a_rcv, in_snd, in_rcv, g_snd, g_rcv, x_snd, x_rcv, y_snd, y_rcv, rs_snd, ag_snd, line_rcv,
                 n_snd, n_rcv, np_snd, np_rcv, nt_snd, nt_rcv, ld, st, vo, loc):
     r = lax.axis_index("data")
     s = lax.axis_index("stage")
@@ -85,10 +86,11 @@
     partner = s + 1 - 2 * (s % 2)
     pair, plane = s // 2, r // 3
     early = EARLY[0] + (EARLY[1] - EARLY[0]) * (s % 2)
+    recv1, own1, sq_o = (first_o.at[i] for i in range(3))
     accs, recvs, owns, gouts = (acc1, acc2), (recv1, recv2), (own1, own2), (g1_o, g2_o)
     rings, weights_hbm, moments_hbm = (ring1, ring2), (w1, w2), (m1, m2)
     heights = (R1, R2)
-    gp, dz = sq_o.at[pl.ds(0, ROWS), :], sq_o.at[pl.ds(ROWS, ROWS), :]
+    gp, dz = first_o.at[2, pl.ds(0, ROWS), :], first_o.at[2, pl.ds(ROWS, ROWS), :]
 
     def remote(src, dst, snd, rcv, to_r, to_s):
         return pltpu.make_async_remote_copy(src_ref=src, dst_ref=dst, send_sem=snd, recv_sem=rcv,
@@ -148,7 +150,7 @@
     def rs_copy(mat, k, src):
         part = recvs[mat].at[ds(k, heights[mat]), :]
         sem = mat * CHUNKS + k
-        return remote(src, part, rs_snd.at[sem], rs_rcv.at[sem], r - away, s)
+        return remote(src, part, rs_snd.at[mat], line_rcv.at[sem], r - away, s)
 
     def rs_src(mat, k):
         return owns[mat].at[ds(k, heights[mat]), :]
@@ -157,7 +159,10 @@
         rows = ds(k, heights[mat])
         src = recvs[mat] if from_vmem else gouts[mat]
         sem = mat * CHUNKS + k
-        return remote(src.at[rows, :], gouts[mat].at[rows, :], ag_snd.at[sem], ag_rcv.at[sem], r + away, s)
+        return remote(src.at[rows, :], gouts[mat].at[rows, :], ag_snd.at[sem // GROUP], line_rcv.at[sem], r + away, s)
+
+    def sent(mat, group):
+        arrive(gouts[mat].at[ds(group, GROUP * heights[mat]), :], ag_snd.at[mat * (CHUNKS // GROUP) + group])
 
     def ag_range(lo, hi):
         for mat in (0, 1):
@@ -196,7 +201,7 @@
             @pl.loop(0, CHUNKS)
             def _(k):
                 rows = ds(k, heights[mat])
-                arrive(recvs[mat].at[rows, :], rs_rcv.at[mat * CHUNKS + k])
+                arrive(recvs[mat].at[rows, :], line_rcv.at[mat * CHUNKS + k])
                 recvs[mat][rows, :] = recvs[mat][rows, :] + owns[mat][rows, :]
                 rs_copy(mat, k, recvs[mat].at[rows, :]).start()
 
@@ -221,13 +226,14 @@
         fills = ([whole(0, w1, recv1, 0), whole(0, m1, own1, 1), whole(0, v1, sq_o, 2)], [whole(1, w2, recv2, 0), whole(1, m2, own2, 1)])
 
         def prefetch():
-            each((0, 1), lambda mat, k: rs_copy(mat, k, rs_src(mat, k)).wait_send())
+            for mat in (0, 1):
+                arrive(recvs[mat], rs_snd.at[mat])
             for copy in fills[0] + fills[1]:
                 copy.start()
 
         def pass_on(mat, k):
             rows = ds(k, heights[mat])
-            arrive(gouts[mat].at[rows, :], ag_rcv.at[mat * CHUNKS + k])
+            arrive(gouts[mat].at[rows, :], line_rcv.at[mat * CHUNKS + k])
 
             @pl.when(d != 3)
             def _():
@@ -254,7 +260,7 @@
         def _():
             arrive(nplane, nt_rcv)
 
-        clip = clip_of(nplane[0] + nplane[1], maxn[...])[0:1, 0:1]
+        clip = clip_of(nplane[0] + nplane[1], maxn[0, 0])[0:1, 0:1]
         for copy in fills[0]:
             copy.wait()
 
@@ -337,7 +343,7 @@
 
         @pl.when(d != 3)
         def _():
-            each((0, 1), lambda mat, k: ag_copy(mat, k, False).wait_send())
+            each((0, 1), sent, 0, CHUNKS // GROUP)
 
     @pl.when(d == 0)
     def _():
@@ -414,7 +420,7 @@
             @pl.loop(0, CHUNKS)
             def _(k):
                 rows = ds(k, heights[mat])
-                arrive(recvs[mat].at[rows, :], rs_rcv.at[mat * CHUNKS + k])
+                arrive(recvs[mat].at[rows, :], line_rcv.at[mat * CHUNKS + k])
                 avg = (recvs[mat][rows, :] + owns[mat][rows, :]) * (1.0 / REPLICAS)
                 recvs[mat][rows, :] = avg
                 part = avg[0:8, :] * avg[0:8, :]
@@ -457,7 +463,7 @@
         norm_copies[-1].start()
         total = nplane[0] + nplane[1]
 
-        clip = clip_of(total, maxn[...])[0:1, 0:1]
+        clip = clip_of(total, maxn[0, 0])[0:1, 0:1]
         for copy in fills:
             copy.wait()
 
@@ -558,7 +564,10 @@
 
         @pl.loop(0, CHUNKS)
         def _(k):
-            ag_copy(0, k, True).wait_send()
+            @pl.when(k % GROUP == 0)
+            def _():
+                sent(0, k // GROUP)
+
             load_rows(0, k, w1.at[0]).wait()
             rows = ds(k, R1)
             recv1[rows, :] = new_weight(ring1[k % SLOTS], own1[rows, :], sq_o[rows, :])
@@ -569,7 +578,10 @@
 
         @pl.loop(0, CHUNKS)
         def _(k):
-            ag_copy(1, k, True).wait_send()
+            @pl.when(k % GROUP == 0)
+            def _():
+                sent(1, k // GROUP)
+
             load_rows(1, k, w2.at[0]).wait()
             load_v2(k, v2_o).wait()
             rows = ds(k, R2)
@@ -590,25 +602,26 @@
             remote(y_o, y_o, y_snd.at[t], y_rcv, r, (s + t) % STAGES).wait_send()
 
 
-def flush_kernel(*refs):
-    source, target, (buf, rsem, wsem) = refs[5], refs[11], refs[12:]
-    keep = pltpu.make_async_copy(refs[4], refs[10], wsem.at[FLUSH])
-    keep.start()
+def flush_kernel(w_second, m_second, first, v_second, w_out, m_out, w_first, m_first, v_first, v_out, buf, rsem, wsem):
     height = FF // FLUSH
 
-    def copies(k):
+    def parts(k):
         rows = pl.ds(k * height, height)
-        return (pltpu.make_async_copy(source.at[rows, :], buf.at[rows, :], rsem.at[k]),
-                pltpu.make_async_copy(buf.at[rows, :], target.at[rows, :], wsem.at[k]))
-
+        return (pltpu.make_async_copy(v_second.at[rows, :], buf.at[rows, :], rsem.at[k]),
+                pltpu.make_async_copy(buf.at[rows, :], v_out.at[rows, :], wsem.at[k]))
+
+    copies = [pltpu.make_async_copy(first.at[i], target, wsem.at[FLUSH + i]) for i, target in enumerate((w_first, m_first, v_first))]
     for k in range(FLUSH):
-        copies(k)[0].start()
+        parts(k)[0].start()
+    for copy in copies:
+        copy.start()
     for k in range(FLUSH):
-        copies(k)[0].wait()
-        copies(k)[1].start()
+        parts(k)[0].wait()
+        parts(k)[1].start()
     for k in range(FLUSH):
-        copies(k)[1].wait()
-    keep.wait()
+        parts(k)[1].wait()
+    for copy in copies:
+        copy.wait()
 
 
 def solution(mesh):
@@ -617,20 +630,20 @@
     acc_spec = P("data", "stage", None, None)
 
     def local_step(w_in, w_out, mom_in, mom_out, sq_in, sq_out, acc_in, acc_out, stage_acts, grad_y, x_next, max_norm):
-        maxn = jnp.full((8, 128), max_norm, F32)
+        maxn = max_norm.reshape(1, 1)
         hbm = pl.BlockSpec(memory_space=pl.ANY)
         vmem = pl.BlockSpec(memory_space=pltpu.VMEM)
         dma = pltpu.SemaphoreType.DMA
-        wide, tall = pltpu.VMEM((D, FF), F32), pltpu.VMEM((FF, D), F32)
-        *kept, sq_out_new, _, _, y_next = pl.pallas_call(
+        tall = pltpu.VMEM((FF, D), F32)
+        w_second, m_second, first, v_second, _, _, y_next = pl.pallas_call(
             step_kernel,
             out_shape=(
-                wide, tall, wide, tall, wide,
+                tall, tall, pltpu.VMEM((3, D, FF), F32),
                 jax.ShapeDtypeStruct((FF, D), F32), jax.ShapeDtypeStruct((D, FF), F32), jax.ShapeDtypeStruct((FF, D), F32),
                 jax.ShapeDtypeStruct((TOK, D), BF16),
             ),
-            in_specs=[hbm] * 11 + [vmem],
-            out_specs=(vmem,) * 5 + (hbm,) * 4,
+            in_specs=[hbm] * 11 + [pl.BlockSpec(memory_space=pltpu.SMEM)],
+            out_specs=(vmem,) * 3 + (hbm,) * 4,
             scratch_shapes=[
                 pltpu.VMEM((D, FF), BF16), pltpu.VMEM((FF, D), BF16), pltpu.VMEM((ROWS, FF), BF16),
                 pltpu.VMEM((SLOTS, R1, FF), F32), pltpu.VMEM((SLOTS, R2, D), F32), pltpu.VMEM((SLOTS, R2, D), F32),
@@ -639,7 +652,7 @@
                 pltpu.VMEM((8, FF), F32), pltpu.VMEM((8, D), F32),
                 pltpu.VMEM((REPLICAS, 8, 128), F32), pltpu.VMEM((2, 8, 128), F32),
                 dma, dma((REPLICAS,)), dma, dma((REPLICAS,)), dma, dma, dma, dma, dma((STAGES + REPLICAS,)), dma,
-                dma((2 * CHUNKS,)), dma((2 * CHUNKS,)), dma((2 * CHUNKS,)), dma((2 * CHUNKS,)),
+                dma((2,)), dma((2 * CHUNKS // GROUP,)), dma((2 * CHUNKS,)),
                 dma((REPLICAS,)), dma((REPLICAS,)), dma((2,)), dma((3,)), dma((REPLICAS,)), dma,
                 dma((2, 4)), dma((3 * SLOTS,)), dma((SLOTS,)), dma((3,)),
             ],
@@ -647,16 +660,17 @@
             name="step",
         )(w_in, w_out, mom_in, mom_out, sq_in, sq_out, acc_in, acc_out, stage_acts[0], grad_y, x_next[0], maxn)
         wide, tall = jax.ShapeDtypeStruct((D, FF), F32), jax.ShapeDtypeStruct((FF, D), F32)
-        new = pl.pallas_call(
+        w_out_new, m_out_new, w_in_new, m_in_new, v_in_new, v_out_new = pl.pallas_call(
             flush_kernel,
-            out_shape=(wide, tall, wide, tall, wide, tall),
-            in_specs=[hbm] * 4 + [vmem, hbm],
+            out_shape=(tall, tall, wide, wide, wide, tall),
+            in_specs=[hbm, hbm, vmem, hbm],
             out_specs=(hbm,) * 6,
-            input_output_aliases={i: i for i in range(4)},
-            scratch_shapes=[pltpu.VMEM((FF, D), F32), dma((FLUSH,)), dma((FLUSH + 1,))],
+            input_output_aliases={0: 0, 1: 1},
+            scratch_shapes=[pltpu.VMEM((FF, D), F32), dma((FLUSH,)), dma((FLUSH + 3,))],
             compiler_params=pltpu.CompilerParams(vmem_limit_bytes=10000000),
             name="flush",
-        )(*kept[:4], pltpu.with_memory_space_constraint(kept[4], pltpu.VMEM), sq_out_new)
+        )(w_second, m_second, pltpu.with_memory_space_constraint(first, pltpu.VMEM), v_second)
+        new = (w_in_new, w_out_new, m_in_new, m_out_new, v_in_new, v_out_new)
         return *(array[None] for array in new), y_next[None]
 
     in_specs = (weight_spec,) * 6 + (acc_spec, acc_spec, P("stage", "data", None), P("data", None), P(None, "data", None), P())

time: 473 us -> 462 us (0.977)
  local copies, waits for them, and re-layouts: 16.2 us -> 8.13 us
    unnamed x7 -> x5, local copies, waits for them, and re-layouts: 15.6 us -> 8.13 us
where the time goes in v4:
time: 462 us; the launch traced here: 457 us
  Pallas kernels  448 us (97%)
  local copies, waits for them, and re-layouts  8.13 us (2%)
    pallas_call x1, Pallas kernels, local_step(): pl.pallas_call(step_kernel, out_shape=(tall, tall, pltpu.VMEM((3, D, FF),...  433 us
    pallas_call x1, Pallas kernels, local_step(): pl.pallas_call(flush_kernel, out_shape=(tall, tall, wide, wide, wide, tal...  15.1 us

profile of v4, /device:TPU:31, one launch (start us, length us, event | category | flops | bytes accessed | tf_op | source)
XLA Modules:
  0.0 457.1 jit_solution(17424704015611871915)
XLA Ops:
  1.3 432.5 %step.1 = (f32[3072,768]{1,0:T(8,128)S(1)}, f32[3072,768]{1,0:T(8,128)S(1)}, f32[3,768,3072]{2,1,0:T(8,128)S(1)}, f32[3072,768]{1,0:T(8,128)}, f32[768,3072]{1,0...) custom-call(f32[1,768,3072]{2,1,0:T(8,128)} %w1.1, f32[1,3072,768]{2,1,0:T(8,128)} %w2.1, f32[1,768,3072]{2,1,0:T(8,128)} %m1.1, ...), custom_call_target="tpu_custom_call" | custom-call | tf_op jit(solution)/shard_map/step/pallas_call | solution.py:638
  433.8 15.1 %flush.1 = (f32[3072,768]{1,0:T(8,128)S(1)}, f32[3072,768]{1,0:T(8,128)S(1)}, f32[768,3072]{1,0:T(8,128)}, f32[768,3072]{1,0:T(8,128)}, f32[768,3072]{1,0:T(8,128)}, /*index=5*/f32[3072,768]{1,0:T(8,128)}) custom-call(f32[3072,768]{1,0:T(8,128)S(1)} %get-tuple-element.18.w_second, ...), custom_call_target="tpu_custom_call", output_to_operand_aliasing={{0}: (0, {}), {1}: (1, {})} | custom-call | tf_op jit(solution)/shard_map/flush/pallas_call | solution.py:663
  448.9 3.7 copy.26
  452.7 0.0 copy-start
  452.7 3.7 copy.27
  456.4 0.0 copy-done
  456.4 0.6 copy.29
Async XLA Ops:
  452.7 3.7 copy-start

commit v5 on v4

--- a/solution.py
+++ b/solution.py
@@ -25,7 +25,8 @@
 LAG = 16
 TILE = 256
 SLOTS = 8
-EARLY = (8, 2)
+EARLY = (9, 2)
+HEAD = (3, 0)
 VMEM_LIMIT = 19800000
 FLUSH = 4
 LEARN_RATE = LR_GAIN * D ** -0.5
@@ -86,6 +87,7 @@
     partner = s + 1 - 2 * (s % 2)
     pair, plane = s // 2, r // 3
     early = EARLY[0] + (EARLY[1] - EARLY[0]) * (s % 2)
+    head = jnp.where(d == 1, HEAD[0] + (HEAD[1] - HEAD[0]) * (s % 2), 0)
     recv1, own1, sq_o = (first_o.at[i] for i in range(3))
     accs, recvs, owns, gouts = (acc1, acc2), (recv1, recv2), (own1, own2), (g1_o, g2_o)
     rings, weights_hbm, moments_hbm = (ring1, ring2), (w1, w2), (m1, m2)
@@ -175,6 +177,14 @@
             @pl.loop(lo, hi)
             def _(k):
                 fn(mat, k)
+
+    def pass_on(mat, k):
+        rows = ds(k, heights[mat])
+        arrive(gouts[mat].at[rows, :], line_rcv.at[mat * CHUNKS + k])
+
+        @pl.when(d != 3)
+        def _():
+            ag_copy(mat, k, False).start()
 
     @pl.when(d == 3)
     def _():
@@ -204,6 +214,10 @@
                 arrive(recvs[mat].at[rows, :], line_rcv.at[mat * CHUNKS + k])
                 recvs[mat][rows, :] = recvs[mat][rows, :] + owns[mat][rows, :]
                 rs_copy(mat, k, recvs[mat].at[rows, :]).start()
+                if mat == 1:
+                    @pl.when(k >= CHUNKS - head)
+                    def _():
+                        pass_on(0, k - (CHUNKS - head))
 
     def load(mat, k, src, ring, sem):
         slot = k % SLOTS
@@ -230,14 +244,6 @@
                 arrive(recvs[mat], rs_snd.at[mat])
             for copy in fills[0] + fills[1]:
                 copy.start()
-
-        def pass_on(mat, k):
-            rows = ds(k, heights[mat])
-            arrive(gouts[mat].at[rows, :], line_rcv.at[mat * CHUNKS + k])
-
-            @pl.when(d != 3)
-            def _():
-                ag_copy(mat, k, False).start()
 
         @pl.when(d == 3)
         def _():
@@ -248,7 +254,7 @@
             for q in (1, 2):
                 remote(nplane, nplane, nt_snd.at[q], nt_rcv, own_r + q * away, s).start()
 
-        each((0,), pass_on, 0, LAG // 2)
+        each((0,), pass_on, head, LAG // 2)
 
         @pl.when(d != 3)
         def _():

time: 462 us -> 458 us (level)
  no operation moved by 1% of the time
where the time goes in v5:
time: 458 us; the launch traced here: 457 us
  Pallas kernels  448 us (98%)
  local copies, waits for them, and re-layouts  8.13 us (2%)
    pallas_call x1, Pallas kernels, local_step(): pl.pallas_call(step_kernel, out_shape=(tall, tall, pltpu.VMEM((3, D, FF),...  433 us
    pallas_call x1, Pallas kernels, local_step(): pl.pallas_call(flush_kernel, out_shape=(tall, tall, wide, wide, wide, tal...  15.1 us

profile of v5, /device:TPU:31, one launch (start us, length us, event | category | flops | bytes accessed | tf_op | source)
XLA Modules:
  0.0 457.1 jit_solution(10061519760340703238)
XLA Ops:
  1.3 432.5 %step.1 = (f32[3072,768]{1,0:T(8,128)S(1)}, f32[3072,768]{1,0:T(8,128)S(1)}, f32[3,768,3072]{2,1,0:T(8,128)S(1)}, f32[3072,768]{1,0:T(8,128)}, f32[768,3072]{1,0...) custom-call(f32[1,768,3072]{2,1,0:T(8,128)} %w1.1, f32[1,3072,768]{2,1,0:T(8,128)} %w2.1, f32[1,768,3072]{2,1,0:T(8,128)} %m1.1, ...), custom_call_target="tpu_custom_call" | custom-call | tf_op jit(solution)/shard_map/step/pallas_call | solution.py:644
  433.8 15.1 %flush.1 = (f32[3072,768]{1,0:T(8,128)S(1)}, f32[3072,768]{1,0:T(8,128)S(1)}, f32[768,3072]{1,0:T(8,128)}, f32[768,3072]{1,0:T(8,128)}, f32[768,3072]{1,0:T(8,128)}, /*index=5*/f32[3072,768]{1,0:T(8,128)}) custom-call(f32[3072,768]{1,0:T(8,128)S(1)} %get-tuple-element.18.w_second, ...), custom_call_target="tpu_custom_call", output_to_operand_aliasing={{0}: (0, {}), {1}: (1, {})} | custom-call | tf_op jit(solution)/shard_map/flush/pallas_call | solution.py:669
  448.9 3.7 copy.26
  452.7 0.0 copy-start
  452.7 3.7 copy.27
  456.4 0.0 copy-done
  456.4 0.6 copy.29
Async XLA Ops:
  452.7 3.7 copy-start

commit v6 on v5

--- a/solution.py
+++ b/solution.py
@@ -27,6 +27,7 @@
 SLOTS = 8
 EARLY = (9, 2)
 HEAD = (3, 0)
+DONOR = 3
 VMEM_LIMIT = 19800000
 FLUSH = 4
 LEARN_RATE = LR_GAIN * D ** -0.5
@@ -130,18 +131,29 @@
     def _():
         pl.semaphore_signal(barrier, inc=1, device_id=(r, STAGES - 1), device_id_type=MESH)
 
+    @pl.when((s == STAGES - 1) & (d == 0))
+    def _():
+        for q in range(1, REPLICAS):
+            pl.semaphore_signal(barrier, inc=1, device_id=(q, DONOR), device_id_type=MESH)
+
     at_end = (r == 0) | (r == REPLICAS - 1)
 
     @pl.when(at_end)
     def _():
         pl.semaphore_signal(barrier, inc=1, device_id=(r, partner), device_id_type=MESH)
 
-    signals = REPLICAS - 1 + jnp.where(at_end, 1, 0) + jnp.where(d == 0, STAGES - 1, 0) + jnp.where(s == STAGES - 1, STAGES - 1, 0)
+    signals = REPLICAS - 1 + jnp.where(at_end, 1, 0) + jnp.where(d == 0, STAGES - 1, 0) + jnp.where(s == STAGES - 1, STAGES - 1, 0) + jnp.where((s == DONOR) & (d != 0), 1, 0)
     pl.semaphore_wait(barrier, signals)
 
     @pl.when(s == STAGES - 1)
     def _():
-        gather(gy_in, gbuf, in_snd, in_rcv)
+        @pl.when(d == 0)
+        def _():
+            pltpu.make_async_copy(gy_in, gbuf.at[ds(r, TOK), :], in_rcv.at[r]).start()
+
+    @pl.when((s == DONOR) & (d != 0))
+    def _():
+        remote(gy_in, gbuf.at[ds(r, TOK), :], in_snd, in_rcv.at[r], 0, STAGES - 1).start()
 
     gather(a_in, abuf, a_snd, a_rcv)
 
@@ -343,7 +355,7 @@
 
         remote(a_in, abuf.at[ds(r, TOK), :], a_snd, a_rcv.at[r], own_r, s).wait_send()
 
-        @pl.when((s == 0) | (s == STAGES - 1))
+        @pl.when((s == 0) | (s == DONOR))
         def _():
             remote(x_in, xbuf.at[ds(r, TOK), :], in_snd, in_rcv.at[r], own_r, s).wait_send()
 

time: 458 us -> 458 us (level)
  no operation moved by 1% of the time
where the time goes in v6:
time: 458 us; the launch traced here: 457 us
  Pallas kernels  447 us (98%)
  local copies, waits for them, and re-layouts  8.13 us (2%)
    pallas_call x1, Pallas kernels, local_step(): pl.pallas_call(step_kernel, out_shape=(tall, tall, pltpu.VMEM((3, D, FF),...  432 us
    pallas_call x1, Pallas kernels, local_step(): pl.pallas_call(flush_kernel, out_shape=(tall, tall, wide, wide, wide, tal...  15.1 us

profile of v6, /device:TPU:31, one launch (start us, length us, event | category | flops | bytes accessed | tf_op | source)
XLA Modules:
  0.0 456.6 jit_solution(10917695756977037140)
XLA Ops:
  1.3 432.1 %step.1 = (f32[3072,768]{1,0:T(8,128)S(1)}, f32[3072,768]{1,0:T(8,128)S(1)}, f32[3,768,3072]{2,1,0:T(8,128)S(1)}, f32[3072,768]{1,0:T(8,128)}, f32[768,3072]{1,0...) custom-call(f32[1,768,3072]{2,1,0:T(8,128)} %w1.1, f32[1,3072,768]{2,1,0:T(8,128)} %w2.1, f32[1,768,3072]{2,1,0:T(8,128)} %m1.1, ...), custom_call_target="tpu_custom_call" | custom-call | tf_op jit(solution)/shard_map/step/pallas_call | solution.py:656
  433.4 15.1 %flush.1 = (f32[3072,768]{1,0:T(8,128)S(1)}, f32[3072,768]{1,0:T(8,128)S(1)}, f32[768,3072]{1,0:T(8,128)}, f32[768,3072]{1,0:T(8,128)}, f32[768,3072]{1,0:T(8,128)}, /*index=5*/f32[3072,768]{1,0:T(8,128)}) custom-call(f32[3072,768]{1,0:T(8,128)S(1)} %get-tuple-element.18.w_second, ...), custom_call_target="tpu_custom_call", output_to_operand_aliasing={{0}: (0, {}), {1}: (1, {})} | custom-call | tf_op jit(solution)/shard_map/flush/pallas_call | solution.py:681
  448.5 3.7 copy.26
  452.2 0.0 copy-start
  452.2 3.7 copy.27
  456.0 0.0 copy-done
  456.0 0.6 copy.29
Async XLA Ops:
  452.2 3.7 copy-start
